TPU v7x, 128 devices: a whole 4x4x4 slice. The times are simulated.
128 devices in a mesh: px: 8 (over x, z_lo), py: 16 (over z_hi, y, core).
Axes of the slice: x: 4, y: 4, z: 4 (z_hi: 2, z_lo: 2; z = z_hi * 2 + z_lo), core: 2. Of those that a mesh axis runs over, the one named last changes fastest.
Arguments:
- velocity: float32 [3, 8, 512, 2048], P(None, None, 'py', 'px'), may hold values from -6 to 6
- thickness: float32 [8, 512, 2048], P(None, 'py', 'px'), may hold values from 1 to 4
- velocity_tendency: float32 [3, 8, 512, 2048], P(None, None, 'py', 'px'), may hold values from -6 to 6
- thickness_tendency: float32 [8, 512, 2048], P(None, 'py', 'px'), may hold values from -0.5 to 0.5
- cell_distance: float32 [3, 512, 2048], P(None, 'py', 'px'), may hold values from 0.5 to 2
- edge_length: float32 [3, 512, 2048], P(None, 'py', 'px'), may hold values from 0.5 to 2
- cell_area: float32 [512, 2048], P('py', 'px'), may hold values from 1 to 4
- kite_area: float32 [2, 3, 512, 2048], P(None, None, 'py', 'px'), may hold values from 0.2 to 0.8
- coriolis: float32 [2, 512, 2048], P(None, 'py', 'px'), may hold values from -1 to 1
Outputs:
- vertex_potential: float32 [2, 8, 512, 2048], P(None, None, 'py', 'px')
- kinetic_energy: float32 [8, 512, 2048], P(None, 'py', 'px')
- cell_potential: float32 [8, 512, 2048], P(None, 'py', 'px')
- edge_potential: float32 [3, 8, 512, 2048], P(None, None, 'py', 'px')
All inputs are finite; a program needn't handle non-finite values.
Results may differ from a plain program's by a relative error of at most 0.00002.
Values sent between devices are 32-bit elements; how exact they have to be, the bound alone decides.
A program may use at most 64 MiB of HBM per device.

v0:
```python
import jax
import jax.numpy as jnp
from jax import lax
from jax.sharding import PartitionSpec as P

SECTIONS = 4


SECTION_STEP = (0.0, 0.5, 0.5, 1.0)
SECTION_WEIGHT = (1.0 / 6.0, 1.0 / 3.0, 1.0 / 3.0, 1.0 / 6.0)
UPWIND_FACTOR = 0.5


def with_halo(cells, sides, width):
    for axis, dim in sides:
        count = lax.axis_size(axis)
        head = lax.slice_in_dim(cells, 0, width, axis=dim)
        tail = lax.slice_in_dim(cells, cells.shape[dim] - width, cells.shape[dim], axis=dim)
        cells = jnp.concatenate(
            [
                lax.ppermute(tail, axis, [(i, (i + 1) % count) for i in range(count)]),
                cells,
                lax.ppermute(head, axis, [((i + 1) % count, i) for i in range(count)]),
            ],
            axis=dim,
        )
    return cells


def offset(padded, margin, first_off, second_off):
    row_count = padded.shape[-2] - 2 * margin
    col_count = padded.shape[-1] - 2 * margin
    return padded[
        ...,
        margin + first_off : margin + first_off + row_count,
        margin + second_off : margin + second_off + col_count,
    ]


def cell_mean(vertex_pad, margin):
    return (
        offset(vertex_pad[0], margin, 0, 0)
        + offset(vertex_pad[1], margin, 0, 0)
        + offset(vertex_pad[0], margin, -1, 0)
        + offset(vertex_pad[0], margin, 0, -1)
        + offset(vertex_pad[1], margin, 0, -1)
        + offset(vertex_pad[1], margin, 1, -1)
    ) / 6.0


def local(
    velocity,
    thickness,
    velocity_tendency,
    thickness_tendency,
    cell_distance,
    edge_length,
    cell_area,
    kite_area,
    coriolis,
):
    levels = thickness.shape[0]
    row_count = thickness.shape[1]
    col_count = thickness.shape[2]
    rim_width = 3
    geometry = jnp.concatenate([cell_distance, 0.25 * cell_distance * edge_length], axis=0)
    geometry_pad = with_halo(geometry, (("px", 2), ("py", 1)), rim_width)
    vertex_geometry = jnp.concatenate(
        [kite_area.reshape(6, row_count, col_count), coriolis], axis=0
    )
    vertex_geometry_pad = with_halo(vertex_geometry, (("px", 2), ("py", 1)), 2)
    kite_used = vertex_geometry_pad[0:6].reshape((2, 3, row_count + 4, col_count + 4))
    coriolis_used = vertex_geometry_pad[6:8]
    triangle_area = jnp.sum(kite_used, axis=1)
    padded_shape = (row_count + 2 * rim_width, col_count + 2 * rim_width)
    joined = jnp.concatenate(
        [
            velocity.reshape(3 * levels, row_count, col_count),
            thickness,
            velocity_tendency.reshape(3 * levels, row_count, col_count),
            thickness_tendency,
        ],
        axis=0,
    )
    joined_pad = with_halo(joined, (("px", 2), ("py", 1)), rim_width)
    base_count = 4 * levels
    vertex_total = jnp.zeros((2,) + thickness.shape, jnp.float32)
    energy_total = jnp.zeros(thickness.shape, jnp.float32)
    cell_total = jnp.zeros(thickness.shape, jnp.float32)
    edge_total = jnp.zeros(velocity.shape, jnp.float32)
    for section_index in range(SECTIONS):
        step_size = SECTION_STEP[section_index]
        weight_now = SECTION_WEIGHT[section_index]
        velocity_pad = joined_pad[0 : 3 * levels].reshape(
            (3, levels) + padded_shape
        ) + step_size * joined_pad[base_count : base_count + 3 * levels].reshape(
            (3, levels) + padded_shape
        )
        thickness_pad = (
            joined_pad[3 * levels : base_count] + step_size * joined_pad[base_count + 3 * levels :]
        )
        inner_velocity = offset(velocity_pad, rim_width, 0, 0)
        edge_flux = velocity_pad * geometry_pad[0:3][:, None]
        circulation_first = (
            offset(edge_flux[0], 1, 0, 0)
            + offset(edge_flux[2], 1, 1, 0)
            - offset(edge_flux[1], 1, 0, 0)
        )
        circulation_second = (
            offset(edge_flux[1], 1, 0, 0)
            - offset(edge_flux[2], 1, 0, 0)
            - offset(edge_flux[0], 1, -1, 1)
        )
        height_first = (
            kite_used[0, 0] * offset(thickness_pad, 1, 0, 0)
            + kite_used[0, 1] * offset(thickness_pad, 1, 1, 0)
            + kite_used[0, 2] * offset(thickness_pad, 1, 0, 1)
        ) / triangle_area[0]
        height_second = (
            kite_used[1, 0] * offset(thickness_pad, 1, 0, 0)
            + kite_used[1, 1] * offset(thickness_pad, 1, 0, 1)
            + kite_used[1, 2] * offset(thickness_pad, 1, -1, 1)
        ) / triangle_area[1]
        potential_first = (coriolis_used[0] + circulation_first / triangle_area[0]) / height_first
        potential_second = (
            coriolis_used[1] + circulation_second / triangle_area[1]
        ) / height_second
        energy_pad = geometry_pad[3:6][:, None] * velocity_pad * velocity_pad
        kinetic = (
            offset(energy_pad[0], rim_width, 0, 0)
            + offset(energy_pad[1], rim_width, 0, 0)
            + offset(energy_pad[2], rim_width, 0, 0)
            + offset(energy_pad[0], rim_width, -1, 0)
            + offset(energy_pad[1], rim_width, 0, -1)
            + offset(energy_pad[2], rim_width, 1, -1)
        ) / cell_area
        wide_pair = jnp.stack([potential_first, potential_second])
        vertex_pair = offset(wide_pair, rim_width - 1, 0, 0)
        cell_pad = cell_mean(wide_pair, 1)
        vertex_margin = 2
        cell_value = offset(cell_pad, 1, 0, 0)
        cell_below = offset(cell_pad, 1, 1, 0)
        cell_right = offset(cell_pad, 1, 0, 1)
        cell_diagonal = offset(cell_pad, 1, -1, 1)
        mean_zero = 0.5 * (
            offset(wide_pair[0], vertex_margin, 0, 0) + offset(wide_pair[1], vertex_margin, 1, -1)
        )
        mean_one = 0.5 * (
            offset(wide_pair[0], vertex_margin, 0, 0) + offset(wide_pair[1], vertex_margin, 0, 0)
        )
        mean_two = 0.5 * (
            offset(wide_pair[1], vertex_margin, 0, 0) + offset(wide_pair[0], vertex_margin, -1, 0)
        )
        grad_zero = (cell_below - cell_value) / cell_distance[0]
        grad_one = (cell_right - cell_value) / cell_distance[1]
        grad_two = (cell_diagonal - cell_value) / cell_distance[2]
        section_edge = jnp.stack(
            [
                mean_zero - UPWIND_FACTOR * inner_velocity[0] * grad_zero,
                mean_one - UPWIND_FACTOR * inner_velocity[1] * grad_one,
                mean_two - UPWIND_FACTOR * inner_velocity[2] * grad_two,
            ]
        )
        vertex_total = vertex_total + weight_now * vertex_pair
        energy_total = energy_total + weight_now * kinetic
        cell_total = cell_total + weight_now * cell_value
        edge_total = edge_total + weight_now * section_edge
    return (vertex_total, energy_total, cell_total, edge_total)


def solution(mesh):
    placed = (
        P(None, None, "py", "px"),
        P(None, "py", "px"),
        P(None, None, "py", "px"),
        P(None, "py", "px"),
        P(None, "py", "px"),
        P(None, "py", "px"),
        P("py", "px"),
        P(None, None, "py", "px"),
        P(None, "py", "px"),
    )
    return jax.shard_map(
        local,
        mesh=mesh,
        in_specs=placed,
        out_specs=(
            P(None, None, "py", "px"),
            P(None, "py", "px"),
            P(None, "py", "px"),
            P(None, None, "py", "px"),
        ),
        check_vma=False,
    )
```

profile of v0, /device:TPU:25, one launch (start us, length us, event | category | flops | bytes accessed | tf_op | source)
XLA Modules:
  0.0 79.6 jit_solution(12069018761177559682)
XLA Ops:
  0.6 1.0 %multiply_multiply_fusion.3 = f32[3,32,256]{2,1,0:T(8,128)S(1)} fusion(f32[3,32,256]{2,1,0:T(8,128)} %param.14, f32[3,32,256]{2,1,0:T(8,128)} %param.13), kind=kLoop, calls=%fused_computation.229 | loop fusion | flops 49152 | bytes 294912 | tf_op jit(solution)/shard_map/mul | solution.py:66
  1.7 1.6 %fusion.104 = (f32[6,32,3]{2,1,0:T(8,128)}, f32[6,32,3]{2,1,0:T(8,128)}) fusion(f32[3,32,256]{2,1,0:T(8,128)} %param.13, f32[3,32,256]{2,1,0:T(8,128)S(1)} %multiply_multiply_fusion.3), kind=kLoop, calls=%fused_computation.227 | loop fusion | flops 1152 | bytes 201216 | tf_op jit(solution)/shard_map/concatenate | solution.py:66
  3.3 1.6 %collective-permute-start.8 = (f32[6,32,3]{2,1,0:T(8,128)}, f32[6,32,3]{2,1,0:T(8,128)}, u32[]{:S(2)}, u32[]{:S(2)}) collective-permute-start(f32[6,32,3]{2,1,0:T(8,128)} %get-tuple-element.74), channel_id=1, source_target_pairs={{0,16},{16,32},{32,48},{48,64},{64,80},{80,96},{96,112},{112,0},{1... | collective-permute-start | bytes 6920 | tf_op jit(solution)/shard_map/ppermute | solution.py:21
  4.9 2.2 %collective-permute-start.9 = (f32[6,32,3]{2,1,0:T(8,128)}, f32[6,32,3]{2,1,0:T(8,128)}, u32[]{:S(2)}, u32[]{:S(2)}) collective-permute-start(f32[6,32,3]{2,1,0:T(8,128)} %get-tuple-element.75), channel_id=1, source_target_pairs={{16,0},{32,16},{48,32},{64,48},{80,64},{96,80},{112,96},{0,112},{1... | collective-permute-start | bytes 6920 | tf_op jit(solution)/shard_map/ppermute | solution.py:23
  7.1 1.7 %fusion.103 = (f32[8,32,2]{2,1,0:T(8,128)}, f32[8,32,2]{2,1,0:T(8,128)}) fusion(f32[6,32,256]{2,1,0:T(8,128)} %bitcast.144, f32[2,32,256]{2,1,0:T(8,128)} %param.17), kind=kLoop, calls=%fused_computation.225 | loop fusion | flops 1024 | bytes 266240 | tf_op jit(solution)/shard_map/concatenate | solution.py:68
  8.8 3.6 %collective-permute-start.1 = (f32[8,32,2]{2,1,0:T(8,128)}, f32[8,32,2]{2,1,0:T(8,128)S(1)}, u32[]{:S(2)}, u32[]{:S(2)}) collective-permute-start(f32[8,32,2]{2,1,0:T(8,128)} %get-tuple-element.73), channel_id=1, source_target_pairs={{16,0},{32,16},{48,32},{64,48},{80,64},{96,80},{112,96},{0,112},{1... | collective-permute-start | bytes 6152 | tf_op jit(solution)/shard_map/ppermute | solution.py:23
  12.4 1.4 %pad_maximum_fusion.1 = f32[64,32,256]{2,1,0:T(8,128)S(1)} fusion(f32[8,32,256]{2,1,0:T(8,128)} %param.12, f32[24,32,256]{2,1,0:T(8,128)S(1)} %bitcast.134, f32[8,32,256]{2,1,0:T(8,128)} %param.10, f32[24,32,256]{2,1,0:T(8,128)} %bitcast.137), kind=kLoop, calls=%fused_computation.4 | loop fusion | flops 1572864 | bytes 4194304 | tf_op jit(solution)/shard_map/concatenate | solution.py:76
  13.8 0.4 fusion.106
  14.2 1.2 %copy.30 = f32[64,32,3]{0,1,2:T(8,128)} copy(f32[64,32,3]{2,1,0:T(8,128)S(1)} %get-tuple-element.35) | data formatting | bytes 49152 | tf_op jit(solution)/shard_map/slice | solution.py:17
  15.5 0.6 slice_bitcast_fusion.28
  16.1 0.6 copy.29
  16.7 1.5 %collective-permute-start.4 = (f32[64,32,3]{0,1,2:T(8,128)S(1)}, f32[64,32,3]{0,1,2:T(8,128)S(1)}, u32[]{:S(2)}, u32[]{:S(2)}) collective-permute-start(f32[64,32,3]{0,1,2:T(8,128)S(1)} %copy.29), channel_id=1, source_target_pairs={{0,16},{16,32},{32,48},{48,64},{64,80},{80,96},{96,112},{112,0},{1... | collective-permute-start | bytes 73736 | tf_op jit(solution)/shard_map/ppermute | solution.py:21
  18.3 0.9 %pad_maximum_fusion.22 = (f32[8,2,260]{2,1,0:T(2,128)S(1)}, f32[8,2,260]{2,1,0:T(2,128)S(1)}) fusion(f32[8,32,2]{2,1,0:T(8,128)S(1)} %collective-permute-done.1, f32[8,32,2]{2,1,0:T(8,128)S(1)} %collective-permute-done, f32[2,32,256]{2,1,0:T(8,128)} %param.17, f32[6,32,256]{2,1,0:T(8,128)S(1)} %bitcast.145), kind=kLoop, calls=%fused_computation.250 | loop fusion | flops 24960 | bytes 299520 | tf_op jit(solution)/shard_map/slice | solution.py:18
  19.1 5.3 %collective-permute-start.2 = (f32[8,2,260]{2,1,0:T(2,128)S(1)}, f32[8,2,260]{2,1,0:T(2,128)S(1)}, u32[]{:S(2)}, u32[]{:S(2)}) collective-permute-start(f32[8,2,260]{2,1,0:T(2,128)S(1)} %get-tuple-element.56), channel_id=1, source_target_pairs={{0,1},{1,2},{2,3},{3,4},{4,5},{5,6},{6,7},{7,8},{8,9},{9,10},{10,1... | collective-permute-start | bytes 49928 | tf_op jit(solution)/shard_map/ppermute | solution.py:21
  24.5 0.9 %pad_maximum_fusion.18 = (f32[6,3,262]{2,1,0:T(4,128)S(1)}, f32[6,3,262]{2,1,0:T(4,128)S(1)}) fusion(f32[6,32,3]{2,1,0:T(8,128)} %collective-permute-done.9, f32[6,32,3]{2,1,0:T(8,128)} %collective-permute-done.8, f32[3,32,256]{2,1,0:T(8,128)S(1)} %multiply_multiply_fusion.3, f32[3,32,256]{2,1,0:T(8,128)S(1)} %copy-done.3), kind=kLoop, calls=%fused_computation.243 | loop fusion | flops 28296 | bytes 238944 | tf_op jit(solution)/shard_map/slice | solution.py:18
  25.4 5.4 %collective-permute-start.10 = (f32[6,3,262]{2,1,0:T(4,128)S(1)}, f32[6,3,262]{2,1,0:T(4,128)S(1)}, u32[]{:S(2)}, u32[]{:S(2)}) collective-permute-start(f32[6,3,262]{2,1,0:T(4,128)S(1)} %get-tuple-element.58), channel_id=1, source_target_pairs={{0,1},{1,2},{2,3},{3,4},{4,5},{5,6},{6,7},{7,8},{8,9},{9,10},{10,1... | collective-permute-start | bytes 56600 | tf_op jit(solution)/shard_map/ppermute | solution.py:21
  30.8 0.5 collective-permute-done.3
  31.3 0.2 pad_maximum_fusion.5
  31.6 0.7 slice_bitcast_fusion.24
  32.4 0.8 slice_bitcast_fusion.25
  33.1 4.7 %collective-permute-done.11 = f32[6,3,262]{2,1,0:T(4,128)S(1)} collective-permute-done((f32[6,3,262]{2,1,0:T(4,128)S(1)}, f32[6,3,262]{2,1,0:T(4,128)S(1)}, u32[]{:S(2)}, u32[]{:S(2)}) %collective-permute-start.11) | collective-permute-done | bytes 18896 | tf_op jit(solution)/shard_map/ppermute | solution.py:23
  37.8 1.9 %pad_maximum_fusion.12 = f32[6,38,262]{2,1,0:T(8,128)} fusion(f32[6,3,262]{2,1,0:T(4,128)S(1)} %collective-permute-done.11, f32[6,32,3]{2,1,0:T(8,128)} %collective-permute-done.9, f32[3,32,256]{2,1,0:T(8,128)S(1)} %copy-done.7, f32[3,32,256]{2,1,0:T(8,128)S(1)} %copy-done.3, f32[6,32,3]{2,1,0:T(8,128)} %collective-permute-done.8, ...), kind=kLoop, calls=%fused_computation.122 | loop fusion | flops 298680 | bytes 477888 | tf_op jit(solution)/shard_map/concatenate | solution.py:19
  39.7 1.0 %copy.31 = f32[64,32,3]{2,1,0:T(8,128)S(1)} copy(f32[64,32,3]{0,1,2:T(8,128)S(1)} %collective-permute-done.4) | data formatting | bytes 49152 | tf_op jit(solution)/shard_map/ppermute | solution.py:21
  40.7 1.8 %copy.32 = f32[64,32,3]{2,1,0:T(8,128)S(1)} copy(f32[64,32,3]{0,1,2:T(8,128)} %collective-permute-done.5) | data formatting | bytes 49152 | tf_op jit(solution)/shard_map/ppermute | solution.py:23
  42.5 1.7 %pad_maximum_fusion.11 = (f32[64,3,262]{2,1,0:T(4,128)S(1)}, f32[64,3,262]{2,1,0:T(4,128)S(1)}) fusion(f32[64,32,3]{2,1,0:T(8,128)S(1)} %copy.32, f32[64,32,3]{2,1,0:T(8,128)S(1)} %copy.31, f32[8,32,256]{2,1,0:T(8,128)S(1)} %copy-done.4, f32[24,32,256]{2,1,0:T(8,128)S(1)} %bitcast.135, f32[8,32,256]{2,1,0:T(8,128)S(1)} %copy-done.5, f32[24,32,256]{2,1,0:T(8,128)} %bitcast.138), kind=kLoop, calls=%fused_computation.119 | loop fusion | flops 503040 | bytes 2548736 | tf_op jit(solution)/shard_map/slice | solution.py:18
  44.2 0.3 collective-permute-start.6
  44.6 0.2 collective-permute-start.7
  44.9 4.4 %collective-permute-done.6 = f32[64,3,262]{2,1,0:T(4,128)S(1)} collective-permute-done((f32[64,3,262]{2,1,0:T(4,128)S(1)}, f32[64,3,262]{2,1,0:T(4,128)S(1)}, u32[]{:S(2)}, u32[]{:S(2)}) %collective-permute-start.6) | collective-permute-done | bytes 201248 | tf_op jit(solution)/shard_map/ppermute | solution.py:21
  49.3 6.1 %collective-permute-done.7 = f32[64,3,262]{2,1,0:T(4,128)S(1)} collective-permute-done((f32[64,3,262]{2,1,0:T(4,128)S(1)}, f32[64,3,262]{2,1,0:T(4,128)S(1)}, u32[]{:S(2)}, u32[]{:S(2)}) %collective-permute-start.7) | collective-permute-done | bytes 201248 | tf_op jit(solution)/shard_map/ppermute | solution.py:23
  55.4 6.1 %pad_maximum_fusion = f32[64,38,262]{2,1,0:T(8,128)S(1)} fusion(f32[64,3,262]{2,1,0:T(4,128)S(1)} %collective-permute-done.7, f32[64,32,3]{2,1,0:T(8,128)S(1)} %copy.32, f32[8,32,256]{2,1,0:T(8,128)S(1)} %copy-done.4, f32[24,32,256]{2,1,0:T(8,128)S(1)} %bitcast.136, f32[8,32,256]{2,1,0:T(8,128)S(1)} %copy-done.5, f32[24,32,256]{2,1,0:T(8,128)S(1)} %bitcast.139, ...), kind=kLoop, calls=%fused_computation | loop fusion | flops 4460288 | bytes 5097472 | tf_op jit(solution)/shard_map/concatenate | solution.py:19
  61.8 0.9 %multiply_multiply_fusion.2 = (f32[3,8,38,262]{3,2,1,0:T(8,128)S(1)}, f32[3,8,38,262]{3,2,1,0:T(8,128)S(1)}, f32[3,8,38,262]{3,2,1,0:T(8,128)S(1)}, f32[3,8,38,2...) fusion(f32[3,38,262]{2,1,0:T(8,128)S(1)} %get-tuple-element.67, ...), kind=kLoop, calls=%fused_computation.3 | loop fusion | flops 2628384 | bytes 7765680 | tf_op jit(solution)/shard_map/mul | solution.py:128
  62.7 0.3 broadcast_multiply_fusion.2
  63.4 0.6 copy-done.10
  64.1 0.9 %fusion.9 = f32[8,36,260]{2,1,0:T(8,128)S(1)} fusion(f32[8,38,262]{2,1,0:T(8,128)S(1)} %get-tuple-element.17, f32[8,38,262]{2,1,0:T(8,128)S(1)} %get-tuple-element.53, f32[8,38,262]{2,1,0:T(8,128)S(1)} %get-tuple-element.52, f32[8,38,262]{2,1,0:T(8,128)S(1)} %get-tuple-element.51, f32[36,260]{1,0:T(8,128)S(1)} %copy-done.10, f32[36,260]{1,0:T(8,128)S(1)} %copy-done.11, ...), kind=kLoop, calls=%fused_computation.52 | loop fusion | flops 823680 | bytes 2283840 | tf_op jit(solution)/shard_map/div | solution.py:125
  65.1 0.9 %fusion.15 = f32[8,36,260]{2,1,0:T(8,128)S(1)} fusion(f32[8,38,262]{2,1,0:T(8,128)S(1)} %get-tuple-element.17, f32[8,38,262]{2,1,0:T(8,128)S(1)} %get-tuple-element.52, f32[8,38,262]{2,1,0:T(8,128)S(1)} %get-tuple-element.53, f32[8,38,262]{2,1,0:T(8,128)S(1)} %get-tuple-element.51, f32[36,260]{1,0:T(8,128)S(1)} %copy-done.14, f32[36,260]{1,0:T(8,128)S(1)} %copy-done.15, ...), kind=kLoop, calls=%fused_computation.61 | loop fusion | flops 823680 | bytes 2283840 | tf_op jit(solution)/shard_map/div | solution.py:124
  66.0 1.8 %fusion.39 = (f32[8,36,260]{2,1,0:T(8,128)S(1)}, f32[8,36,260]{2,1,0:T(8,128)S(1)}) fusion(f32[8,38,262]{2,1,0:T(8,128)S(1)} %get-tuple-element.16, f32[8,38,262]{2,1,0:T(8,128)S(1)} %get-tuple-element.46, f32[8,38,262]{2,1,0:T(8,128)S(1)} %get-tuple-element.47, f32[8,38,262]{2,1,0:T(8,128)S(1)} %get-tuple-element.45, f32[36,260]{1,0:T(8,128)S(1)} %copy-done.14, ...), kind=kLoop, calls=%fused_computation.101 | loop fusion | flops 1647360 | bytes 4380480 | tf_op jit(solution)/shard_map/div | solution.py:124
  67.7 1.7 %fusion.33 = (f32[8,36,260]{2,1,0:T(8,128)S(1)}, f32[8,36,260]{2,1,0:T(8,128)S(1)}) fusion(f32[8,38,262]{2,1,0:T(8,128)S(1)} %get-tuple-element.16, f32[8,38,262]{2,1,0:T(8,128)S(1)} %get-tuple-element.47, f32[8,38,262]{2,1,0:T(8,128)S(1)} %get-tuple-element.46, f32[8,38,262]{2,1,0:T(8,128)S(1)} %get-tuple-element.45, f32[36,260]{1,0:T(8,128)S(1)} %copy-done.10, ...), kind=kLoop, calls=%fused_computation.92 | loop fusion | flops 1647360 | bytes 4380480 | tf_op jit(solution)/shard_map/div | solution.py:125
  69.5 0.5 fusion.5
  70.0 0.5 fusion.7
  70.4 0.2 copy-done.20
  70.7 0.9 %fusion.60 = (f32[1,8,32,256]{3,2,1,0:T(8,128)S(1)}, f32[1,8,32,256]{3,2,1,0:T(8,128)S(1)}, f32[1,8,32,256]{3,2,1,0:T(8,128)S(1)}) fusion(f32[8,34,258]{2,1,0:T(8,128)S(1)} %fusion.5, f32[3,8,38,262]{3,2,1,0:T(8,128)S(1)} %get-tuple-element.24, f32[8,36,260]{2,1,0:T(8,128)S(1)} %fusion.9, f32[8,36,260]{2,1,0:T(8,128)S(1)} %fusion.15, ...), kind=kLoop, calls=%fused_computation.145 | loop fusion | flops 1376256 | bytes 3768320 | tf_op jit(solution)/shard_map/stack | solution.py:157
  71.6 0.9 %fusion.94 = (f32[1,8,32,256]{3,2,1,0:T(8,128)S(1)}, f32[1,8,32,256]{3,2,1,0:T(8,128)S(1)}, f32[1,8,32,256]{3,2,1,0:T(8,128)S(1)}) fusion(f32[8,34,258]{2,1,0:T(8,128)S(1)} %fusion.7, f32[3,8,38,262]{3,2,1,0:T(8,128)S(1)} %get-tuple-element.9, f32[8,36,260]{2,1,0:T(8,128)S(1)} %get-tuple-element.70, f32[8,36,260]{2,1,0:T(8,128)S(1)} %get-tuple-element.68, ...), kind=kLoop, calls=%fused_computation.195 | loop fusion | flops 1376256 | bytes 3768320 | tf_op jit(solution)/shard_map/stack | solution.py:157
  72.4 0.5 fusion.6
  72.9 0.9 %fusion.77 = (f32[1,8,32,256]{3,2,1,0:T(8,128)S(1)}, f32[1,8,32,256]{3,2,1,0:T(8,128)S(1)}, f32[1,8,32,256]{3,2,1,0:T(8,128)S(1)}) fusion(f32[8,34,258]{2,1,0:T(8,128)S(1)} %fusion.6, f32[3,8,38,262]{3,2,1,0:T(8,128)S(1)} %get-tuple-element.22, f32[8,36,260]{2,1,0:T(8,128)S(1)} %get-tuple-element.71, f32[8,36,260]{2,1,0:T(8,128)S(1)} %get-tuple-element.69, ...), kind=kLoop, calls=%fused_computation.170 | loop fusion | flops 1376256 | bytes 3768320 | tf_op jit(solution)/shard_map/stack | solution.py:157
  73.8 1.0 %fusion.45 = f32[8,32,256]{2,1,0:T(8,128)} fusion(f32[8,34,258]{2,1,0:T(8,128)S(1)} %fusion.5, f32[8,34,258]{2,1,0:T(8,128)S(1)} %fusion.6, f32[8,34,258]{2,1,0:T(8,128)S(1)} %fusion.7), kind=kLoop, calls=%fused_computation.124 | loop fusion | flops 393216 | bytes 1048576 | tf_op jit(solution)/shard_map/add | solution.py:166
  75.1 1.4 %fusion.1 = f32[2,8,32,256]{3,2,1,0:T(8,128)} fusion(f32[1,8,36,260]{3,2,1,0:T(8,128)S(1)} %bitcast.128, f32[1,8,36,260]{3,2,1,0:T(8,128)S(1)} %bitcast.129, f32[1,8,36,260]{3,2,1,0:T(8,128)S(1)} %bitcast.133, f32[1,8,36,260]{3,2,1,0:T(8,128)S(1)} %bitcast.131, f32[1,8,36,260]{3,2,1,0:T(8,128)S(1)} %bitcast.132, f32[1,8,36,260]{3,2,1,0:T(8,128)S(1)} %bitcast.130), kind=kLoop, calls=%fused_computation.16 | loop fusion | flops 1179648 | bytes 2321408 | tf_op jit(solution)/shard_map/add | solution.py:164
  76.5 1.1 %fusion = f32[3,8,32,256]{3,2,1,0:T(8,128)} fusion(f32[1,8,32,256]{3,2,1,0:T(8,128)S(1)} %get-tuple-element.32, f32[1,8,32,256]{3,2,1,0:T(8,128)S(1)} %get-tuple-element.33, f32[1,8,32,256]{3,2,1,0:T(8,128)S(1)} %get-tuple-element.31, f32[1,8,32,256]{3,2,1,0:T(8,128)S(1)} %get-tuple-element.29, f32[1,8,32,256]{3,2,1,0:T(8,128)S(1)} %get-tuple-element.30, ...), kind=kLoop, calls=%fused_computation.8 | loop fusion | flops 2359296 | bytes 3145728 | tf_op jit(solution)/shard_map/add | solution.py:167
  77.6 2.0 %fusion.44 = f32[8,32,256]{2,1,0:T(8,128)} fusion(f32[8,38,262]{2,1,0:T(8,128)S(1)} %get-tuple-element.43, f32[8,38,262]{2,1,0:T(8,128)S(1)} %get-tuple-element.44, f32[8,38,262]{2,1,0:T(8,128)S(1)} %get-tuple-element.42, f32[8,38,262]{2,1,0:T(8,128)S(1)} %get-tuple-element.85, f32[8,38,262]{2,1,0:T(8,128)S(1)} %get-tuple-element.84, ...), kind=kLoop, calls=%fused_computation.123 | loop fusion | flops 1572864 | bytes 5013504 | tf_op jit(solution)/shard_map/add | solution.py:165
  (65 shorter events, 1.2 us)
Async XLA Ops:
  0.6 11.8 %copy-start = (f32[3,8,32,256]{3,2,1,0:T(8,128)S(1)}, f32[3,8,32,256]{3,2,1,0:T(8,128)}, u32[]{:S(2)}) copy-start(f32[3,8,32,256]{3,2,1,0:T(8,128)} %param.11) | copy-start | bytes 2359300
  1.7 22.8 %copy-start.6 = (f32[3,32,256]{2,1,0:T(8,128)}, f32[3,32,256]{2,1,0:T(8,128)S(1)}, u32[]{:S(2)}) copy-start(f32[3,32,256]{2,1,0:T(8,128)S(1)} %multiply_multiply_fusion.3) | copy-start | bytes 294916
  3.3 21.2 %collective-permute-start.8 = (f32[6,32,3]{2,1,0:T(8,128)}, f32[6,32,3]{2,1,0:T(8,128)}, u32[]{:S(2)}, u32[]{:S(2)}) collective-permute-start(f32[6,32,3]{2,1,0:T(8,128)} %get-tuple-element.74), channel_id=1, source_target_pairs={{0,16},{16,32},{32,48},{48,64},{64,80},{80,96},{96,112},{112,0},{1... | collective-permute-start | bytes 6920 | tf_op jit(solution)/shard_map/ppermute | solution.py:21
  4.9 19.5 %collective-permute-start.9 = (f32[6,32,3]{2,1,0:T(8,128)}, f32[6,32,3]{2,1,0:T(8,128)}, u32[]{:S(2)}, u32[]{:S(2)}) collective-permute-start(f32[6,32,3]{2,1,0:T(8,128)} %get-tuple-element.75), channel_id=1, source_target_pairs={{16,0},{32,16},{48,32},{64,48},{80,64},{96,80},{112,96},{0,112},{1... | collective-permute-start | bytes 6920 | tf_op jit(solution)/shard_map/ppermute | solution.py:23
  8.8 7.9 %collective-permute-start = (f32[8,32,2]{2,1,0:T(8,128)}, f32[8,32,2]{2,1,0:T(8,128)S(1)}, u32[]{:S(2)}, u32[]{:S(2)}) collective-permute-start(f32[8,32,2]{2,1,0:T(8,128)} %get-tuple-element.72), channel_id=1, source_target_pairs={{0,16},{16,32},{32,48},{48,64},{64,80},{80,96},{96,112},{112,0},{1... | collective-permute-start | bytes 6152 | tf_op jit(solution)/shard_map/ppermute | solution.py:21
  8.8 9.4 %collective-permute-start.1 = (f32[8,32,2]{2,1,0:T(8,128)}, f32[8,32,2]{2,1,0:T(8,128)S(1)}, u32[]{:S(2)}, u32[]{:S(2)}) collective-permute-start(f32[8,32,2]{2,1,0:T(8,128)} %get-tuple-element.73), channel_id=1, source_target_pairs={{16,0},{32,16},{48,32},{64,48},{80,64},{96,80},{112,96},{0,112},{1... | collective-permute-start | bytes 6152 | tf_op jit(solution)/shard_map/ppermute | solution.py:23
  13.8 1.6 %copy-start.3 = (f32[3,32,256]{2,1,0:T(8,128)S(1)}, f32[3,32,256]{2,1,0:T(8,128)}, u32[]{:S(2)}) copy-start(f32[3,32,256]{2,1,0:T(8,128)} %param.13) | copy-start | bytes 294916
  14.2 4.1 %copy-start.2 = (f32[2,3,32,256]{3,2,1,0:T(8,128)S(1)}, f32[2,3,32,256]{3,2,1,0:T(8,128)}, u32[]{:S(2)}) copy-start(f32[2,3,32,256]{3,2,1,0:T(8,128)} %param.16) | copy-start | bytes 589828
  15.5 15.9 %copy-start.9 = (f32[2,32,256]{2,1,0:T(8,128)S(1)}, f32[2,32,256]{2,1,0:T(8,128)}, u32[]{:S(2)}) copy-start(f32[2,32,256]{2,1,0:T(8,128)} %param.17) | copy-start | bytes 196612
  15.5 25.2 %collective-permute-start.5 = (f32[64,32,3]{0,1,2:T(8,128)}, f32[64,32,3]{0,1,2:T(8,128)}, u32[]{:S(2)}, u32[]{:S(2)}) collective-permute-start(f32[64,32,3]{0,1,2:T(8,128)} %copy.30), channel_id=1, source_target_pairs={{16,0},{32,16},{48,32},{64,48},{80,64},{96,80},{112,96},{0,112},{1... | collective-permute-start | bytes 73736 | tf_op jit(solution)/shard_map/ppermute | solution.py:23
  16.7 22.9 %collective-permute-start.4 = (f32[64,32,3]{0,1,2:T(8,128)S(1)}, f32[64,32,3]{0,1,2:T(8,128)S(1)}, u32[]{:S(2)}, u32[]{:S(2)}) collective-permute-start(f32[64,32,3]{0,1,2:T(8,128)S(1)} %copy.29), channel_id=1, source_target_pairs={{0,16},{16,32},{32,48},{48,64},{64,80},{80,96},{96,112},{112,0},{1... | collective-permute-start | bytes 73736 | tf_op jit(solution)/shard_map/ppermute | solution.py:21
  19.1 11.7 %collective-permute-start.2 = (f32[8,2,260]{2,1,0:T(2,128)S(1)}, f32[8,2,260]{2,1,0:T(2,128)S(1)}, u32[]{:S(2)}, u32[]{:S(2)}) collective-permute-start(f32[8,2,260]{2,1,0:T(2,128)S(1)} %get-tuple-element.56), channel_id=1, source_target_pairs={{0,1},{1,2},{2,3},{3,4},{4,5},{5,6},{6,7},{7,8},{8,9},{9,10},{10,1... | collective-permute-start | bytes 49928 | tf_op jit(solution)/shard_map/ppermute | solution.py:21
  24.5 6.9 %collective-permute-start.3 = (f32[8,2,260]{2,1,0:T(2,128)S(1)}, f32[8,2,260]{2,1,0:T(2,128)S(1)}, u32[]{:S(2)}, u32[]{:S(2)}) collective-permute-start(f32[8,2,260]{2,1,0:T(2,128)S(1)} %get-tuple-element.57), channel_id=1, source_target_pairs={{1,0},{2,1},{3,2},{4,3},{5,4},{6,5},{7,6},{8,7},{9,8},{10,9},{11,1... | collective-permute-start | bytes 49928 | tf_op jit(solution)/shard_map/ppermute | solution.py:23
  25.4 7.8 %collective-permute-start.10 = (f32[6,3,262]{2,1,0:T(4,128)S(1)}, f32[6,3,262]{2,1,0:T(4,128)S(1)}, u32[]{:S(2)}, u32[]{:S(2)}) collective-permute-start(f32[6,3,262]{2,1,0:T(4,128)S(1)} %get-tuple-element.58), channel_id=1, source_target_pairs={{0,1},{1,2},{2,3},{3,4},{4,5},{5,6},{6,7},{7,8},{8,9},{9,10},{10,1... | collective-permute-start | bytes 56600 | tf_op jit(solution)/shard_map/ppermute | solution.py:21
  30.8 7.0 %collective-permute-start.11 = (f32[6,3,262]{2,1,0:T(4,128)S(1)}, f32[6,3,262]{2,1,0:T(4,128)S(1)}, u32[]{:S(2)}, u32[]{:S(2)}) collective-permute-start(f32[6,3,262]{2,1,0:T(4,128)S(1)} %get-tuple-element.59), channel_id=1, source_target_pairs={{1,0},{2,1},{3,2},{4,3},{5,4},{6,5},{7,6},{8,7},{9,8},{10,9},{11,1... | collective-permute-start | bytes 56600 | tf_op jit(solution)/shard_map/ppermute | solution.py:23
  31.6 6.2 %copy-start.7 = (f32[3,32,256]{2,1,0:T(8,128)S(1)}, f32[3,32,256]{2,1,0:T(8,128)}, u32[]{:S(2)}) copy-start(f32[3,32,256]{2,1,0:T(8,128)} %copy-done.6) | copy-start | bytes 294916
  33.1 9.3 %copy-start.4 = (f32[8,32,256]{2,1,0:T(8,128)S(1)}, f32[8,32,256]{2,1,0:T(8,128)}, u32[]{:S(2)}) copy-start(f32[8,32,256]{2,1,0:T(8,128)} %param.12) | copy-start | bytes 786436
  33.1 9.3 %copy-start.5 = (f32[8,32,256]{2,1,0:T(8,128)S(1)}, f32[8,32,256]{2,1,0:T(8,128)}, u32[]{:S(2)}) copy-start(f32[8,32,256]{2,1,0:T(8,128)} %param.10) | copy-start | bytes 786436
  42.5 2.3 %copy-start.8 = (f32[6,38,262]{2,1,0:T(8,128)S(1)}, f32[6,38,262]{2,1,0:T(8,128)}, u32[]{:S(2)}) copy-start(f32[6,38,262]{2,1,0:T(8,128)} %pad_maximum_fusion.12) | copy-start | bytes 716836
  42.5 12.9 %copy-start.1 = (f32[3,8,32,256]{3,2,1,0:T(8,128)S(1)}, f32[3,8,32,256]{3,2,1,0:T(8,128)}, u32[]{:S(2)}) copy-start(f32[3,8,32,256]{3,2,1,0:T(8,128)} %param.9) | copy-start | bytes 2359300
  44.2 5.1 %collective-permute-start.6 = (f32[64,3,262]{2,1,0:T(4,128)S(1)}, f32[64,3,262]{2,1,0:T(4,128)S(1)}, u32[]{:S(2)}, u32[]{:S(2)}) collective-permute-start(f32[64,3,262]{2,1,0:T(4,128)S(1)} %get-tuple-element.14), channel_id=1, source_target_pairs={{0,1},{1,2},{2,3},{3,4},{4,5},{5,6},{6,7},{7,8},{8,9},{9,10},{10,1... | collective-permute-start | bytes 603656 | tf_op jit(solution)/shard_map/ppermute | solution.py:21
  44.6 10.8 %collective-permute-start.7 = (f32[64,3,262]{2,1,0:T(4,128)S(1)}, f32[64,3,262]{2,1,0:T(4,128)S(1)}, u32[]{:S(2)}, u32[]{:S(2)}) collective-permute-start(f32[64,3,262]{2,1,0:T(4,128)S(1)} %get-tuple-element.15), channel_id=1, source_target_pairs={{1,0},{2,1},{3,2},{4,3},{5,4},{6,5},{7,6},{8,7},{9,8},{10,9},{11,1... | collective-permute-start | bytes 603656 | tf_op jit(solution)/shard_map/ppermute | solution.py:23
  63.2 0.8 %copy-start.10 = (f32[36,260]{1,0:T(8,128)S(1)}, f32[36,260]{1,0:T(8,128)}, u32[]{:S(2)}) copy-start(f32[36,260]{1,0:T(8,128)} %get-tuple-element.61) | copy-start | bytes 112324
  63.2 0.9 %copy-start.11 = (f32[36,260]{1,0:T(8,128)S(1)}, f32[36,260]{1,0:T(8,128)}, u32[]{:S(2)}) copy-start(f32[36,260]{1,0:T(8,128)} %get-tuple-element.62) | copy-start | bytes 112324
  63.2 0.9 %copy-start.12 = (f32[36,260]{1,0:T(8,128)S(1)}, f32[36,260]{1,0:T(8,128)}, u32[]{:S(2)}) copy-start(f32[36,260]{1,0:T(8,128)} %get-tuple-element.63) | copy-start | bytes 112324
  63.2 0.9 %copy-start.16 = (f32[36,260]{1,0:T(8,128)S(1)}, f32[36,260]{1,0:T(8,128)}, u32[]{:S(2)}) copy-start(f32[36,260]{1,0:T(8,128)} %get-tuple-element.80) | copy-start | bytes 112324
  63.2 0.9 %copy-start.17 = (f32[36,260]{1,0:T(8,128)S(1)}, f32[36,260]{1,0:T(8,128)}, u32[]{:S(2)}) copy-start(f32[36,260]{1,0:T(8,128)} %get-tuple-element.90) | copy-start | bytes 112324
  64.1 0.9 %copy-start.13 = (f32[36,260]{1,0:T(8,128)S(1)}, f32[36,260]{1,0:T(8,128)}, u32[]{:S(2)}) copy-start(f32[36,260]{1,0:T(8,128)} %get-tuple-element.60) | copy-start | bytes 112324
  64.1 0.9 %copy-start.14 = (f32[36,260]{1,0:T(8,128)S(1)}, f32[36,260]{1,0:T(8,128)}, u32[]{:S(2)}) copy-start(f32[36,260]{1,0:T(8,128)} %get-tuple-element.64) | copy-start | bytes 112324
  64.1 0.9 %copy-start.15 = (f32[36,260]{1,0:T(8,128)S(1)}, f32[36,260]{1,0:T(8,128)}, u32[]{:S(2)}) copy-start(f32[36,260]{1,0:T(8,128)} %get-tuple-element.65) | copy-start | bytes 112324
  64.1 0.9 %copy-start.18 = (f32[36,260]{1,0:T(8,128)S(1)}, f32[36,260]{1,0:T(8,128)}, u32[]{:S(2)}) copy-start(f32[36,260]{1,0:T(8,128)} %get-tuple-element.79) | copy-start | bytes 112324
  64.1 0.9 %copy-start.19 = (f32[36,260]{1,0:T(8,128)S(1)}, f32[36,260]{1,0:T(8,128)}, u32[]{:S(2)}) copy-start(f32[36,260]{1,0:T(8,128)} %get-tuple-element.91) | copy-start | bytes 112324
  69.9 0.8 copy-start.20
  69.9 0.8 copy-start.21
  76.5 1.1 %copy-start.22 = (f32[32,256]{1,0:T(8,128)S(1)}, f32[32,256]{1,0:T(8,128)}, u32[]{:S(2)}) copy-start(f32[32,256]{1,0:T(8,128)} %param.15) | copy-start | bytes 98308
where the time goes:
time: 80.2 us; the launch traced here: 79.6 us
  other arithmetic  34.3 us (43%)
  starting transfers between devices  20.2 us (25%)
  waiting for transfers between devices  15.7 us (20%)
  local copies, waits for them, and re-layouts  8.22 us (10%)
  between operations  1.05 us (1%)
    ppermute x6, starting transfers between devices, with_halo(): lax.ppermute(tail, axis, [(i, (i + 1) % count) for i in range(count)])  14.2 us
    ppermute x6, waiting for transfers between devices, with_halo(): lax.ppermute(head, axis, [((i + 1) % count, i) for i in range(count)])  11.3 us
    concatenate x3, other arithmetic, with_halo(): jnp.concatenate([lax.ppermute(tail, axis, [(i, (i + 1) % count) for i in...  8.24 us
    ppermute x6, starting transfers between devices, with_halo(): lax.ppermute(head, axis, [((i + 1) % count, i) for i in range(count)])  6.02 us
    ppermute x6, waiting for transfers between devices, with_halo(): lax.ppermute(tail, axis, [(i, (i + 1) % count) for i in range(count)])  4.46 us
    slice x3, other arithmetic, with_halo(): lax.slice_in_dim(cells, cells.shape[dim] - width, cells.shape[dim], axis=...  3.5 us
    div x2, other arithmetic, local(): (coriolis_used[0] + circulation_first / triangle_area[0]) / height_first  2.66 us
    another operation x3, other arithmetic, local(): jnp.stack([mean_zero - UPWIND_FACTOR * inner_velocity[0] * grad_zero, mea...  2.59 us
  transfers between devices with their start and end apart: 12, of which 4 were waited for; matrix products, arithmetic and copies ran while one was open for 16% of the time, Pallas kernels for 0%

commit v1 on v0

v1 whole, which is shorter than its diff:
```python
import jax
import jax.numpy as jnp
from jax import lax
from jax.experimental import pallas as pl
from jax.experimental.pallas import tpu as pltpu
from jax.sharding import PartitionSpec as P

F32 = jnp.float32
MESH = pl.DeviceIdType.MESH
ROWS = 32
EXT = ROWS + 4
LEVELS = 8
LANES = 128

FIRST = (-2, 12, 26)
FIELDS = 10

DOWN, UP, RIGHT, LEFT = (1, 0), (-1, 0), (0, 1), (0, -1)
DOWN_LEFT, UP_LEFT, UP_RIGHT = (1, -1), (-1, -1), (-1, 1)
TARGETS = (DOWN, UP, RIGHT, LEFT, DOWN_LEFT, UP_LEFT, UP_RIGHT)


def rim_of(row):
    block = 0 if row <= 12 else (1 if row <= 26 else 2)
    return block, (row - FIRST[block]) * 8


def lane_id():
    return lax.broadcasted_iota(jnp.int32, (LEVELS, LANES), 1)


def turn(x, amount):
    amount = amount % LANES
    return x if amount == 0 else pltpu.roll(x, amount, 1)


def next_col(pair, lane):
    first, second = turn(pair[0], -1), turn(pair[1], -1)
    return jnp.where(lane == LANES - 1, second, first), second


def prev_col(pair, lane):
    first, second = turn(pair[0], 1), turn(pair[1], 1)
    return first, jnp.where(lane == 0, first, second)


def tile(t):
    return pl.ds(t * LANES, LANES)


def row_pair(ref, *index):
    return ref[(*index, slice(None), tile(0))], ref[(*index, slice(None), tile(1))]


def spread(ref, row, plane, t):
    return jnp.broadcast_to(ref[row, pl.ds(plane, 1), tile(t)], (LEVELS, LANES))


def spread_pair(ref, row, plane):
    return spread(ref, row, plane, 0), spread(ref, row, plane, 1)


def both(fn, *pairs):
    return tuple(fn(*(p[t] for p in pairs)) for t in range(2))


def weigh(n0, n1, s0, s1):
    start = n0 / s0
    middle = (n0 + n0 + n1) / (s0 + s0 + s1)
    end = (n0 + n1) / (s0 + s1)
    twice = middle + middle
    late = twice + end
    return (start + twice + late) * (1.0 / 6.0), late * (1.0 / 6.0)


def first_vertex(cor, k0, k1, k2, f0, f1, f2_down, g0, g1, g2_down, h, h_down, h_right, m, m_down, m_right):
    n0 = cor * (k0 + k1 + k2) + (f0 + f2_down - f1)
    n1 = g0 + g2_down - g1
    s0 = k0 * h + k1 * h_down + k2 * h_right
    s1 = k0 * m + k1 * m_down + k2 * m_right
    return weigh(n0, n1, s0, s1)


def second_vertex(cor, k0, k1, k2, f1, f2, f0_diag, g1, g2, g0_diag, h, h_right, h_diag, m, m_right, m_diag):
    n0 = cor * (k0 + k1 + k2) + (f1 - f2 - f0_diag)
    n1 = g1 - g2 - g0_diag
    s0 = k0 * h + k1 * h_right + k2 * h_diag
    s1 = k0 * m + k1 * m_right + k2 * m_diag
    return weigh(n0, n1, s0, s1)


def energy_of(v, w, d, e):
    return (v * (v + w) + (w * w) * (1.0 / 3.0)) * (0.25 * d * e)


def vertices(lo, hi, v, h, w, m, ga, gb, out):
    def flux(ref, k, row):
        return both(lambda a, d: a * d, row_pair(ref, k, row), spread_pair(ga, row, k))

    def right_of(row):
        lane = lane_id()
        return (
            next_col(flux(v, 0, row), lane)
            + next_col(flux(w, 0, row), lane)
            + next_col(row_pair(h, row), lane)
            + next_col(row_pair(m, row), lane)
        )

    def body(row, carry):
        lane = lane_id()
        f0_diag, g0_diag, h_diag, m_diag = (carry[i : i + 2] for i in (0, 2, 4, 6))
        f2, g2, hh, mm = (carry[i : i + 2] for i in (8, 10, 12, 14))
        below = jnp.minimum(row + 1, EXT - 1)
        d0, d1 = spread_pair(ga, row, 0), spread_pair(ga, row, 1)
        mul = lambda a, d: a * d
        f0 = both(mul, row_pair(v, 0, row), d0)
        f1 = both(mul, row_pair(v, 1, row), d1)
        g0 = both(mul, row_pair(w, 0, row), d0)
        g1 = both(mul, row_pair(w, 1, row), d1)
        f2_down, g2_down = flux(v, 2, below), flux(w, 2, below)
        h_down, m_down = row_pair(h, below), row_pair(m, below)
        f0_right, g0_right = next_col(f0, lane), next_col(g0, lane)
        h_right, m_right = next_col(hh, lane), next_col(mm, lane)
        kite = [spread_pair(gb, row, p) for p in range(6)]
        cor0, cor1 = spread_pair(ga, row, 4), spread_pair(ga, row, 5)
        for t in range(2):
            a, b = first_vertex(
                cor0[t], kite[0][t], kite[1][t], kite[2][t], f0[t], f1[t], f2_down[t], g0[t], g1[t], g2_down[t],
                hh[t], h_down[t], h_right[t], mm[t], m_down[t], m_right[t],
            )
            out[0, row, :, tile(t)] = a
            out[1, row, :, tile(t)] = b
            a, b = second_vertex(
                cor1[t], kite[3][t], kite[4][t], kite[5][t], f1[t], f2[t], f0_diag[t], g1[t], g2[t], g0_diag[t],
                hh[t], h_right[t], h_diag[t], mm[t], m_right[t], m_diag[t],
            )
            out[2, row, :, tile(t)] = a
            out[3, row, :, tile(t)] = b
        return f0_right + g0_right + h_right + m_right + f2_down + g2_down + h_down + m_down

    start = right_of(max(lo - 1, 0)) + flux(v, 2, lo) + flux(w, 2, lo) + row_pair(h, lo) + row_pair(m, lo)
    lax.fori_loop(lo, hi, body, start)


def cells(lo, hi, sums, out):
    def body(row, _):
        lane = lane_id()
        for n in range(2):
            v0, v1 = row_pair(sums, n, row), row_pair(sums, 2 + n, row)
            above, below = row_pair(sums, n, row - 1), row_pair(sums, 2 + n, row + 1)
            here = both(lambda a, b: a + b, v0, v1)
            left = prev_col(both(lambda a, b: a + b, here, below), lane)
            for t in range(2):
                out[n, row, :, tile(t)] = (here[t] + above[t] + left[t]) * (1.0 / 6.0)
        return 0

    lax.fori_loop(lo, hi, body, 0)


def energies(lo, hi, v, w, ga, gb, inverse, out):
    spots = ((ga, 6), (ga, 7), (gb, 6))

    def one(k, row):
        ref, plane = spots[k]
        return both(energy_of, row_pair(v, k, row), row_pair(w, k, row), spread_pair(ga, row, k), spread_pair(ref, row, plane))

    def body(row, carry):
        lane = lane_id()
        above, e2 = carry[0:2], carry[2:4]
        e0, e1, e2_down = one(0, row), one(1, row), one(2, row + 1)
        left = prev_col(both(lambda a, b: a + b, e1, e2_down), lane)
        area = spread_pair(inverse, row, 3)
        for t in range(2):
            out[row - 2, :, tile(t)] = (e0[t] + e1[t] + e2[t] + above[t] + left[t]) * area[t]
        return e0 + e2_down

    lax.fori_loop(lo, hi, body, one(0, lo - 1) + one(2, lo))


def exchange_kernel(
    v_in, h_in, w_in, m_in, cd_in, el_in, ca_in, ka_in, co_in,
    v, w, sums, cell, kin, inverse, rim_v, rim_c, rim_k,
    h, m, ga, gb, own, to_right, to_left, from_left, from_right, corner_tr, corner_br, corner_bl, rim,
    load_sem, send_sem, recv_sem,
):
    ny, nx = lax.axis_size("py"), lax.axis_size("px")
    my, mx = lax.axis_index("py"), lax.axis_index("px")

    def device(dy, dx):
        return {"py": lax.rem(my + dy + ny, ny), "px": lax.rem(mx + dx + nx, nx)}

    barrier = pltpu.get_barrier_semaphore()
    for dy, dx in TARGETS:
        pl.semaphore_signal(barrier, inc=1, device_id=device(-dy, -dx), device_id_type=MESH)

    loads = []

    def load(src, dst):
        loads.append(pltpu.make_async_copy(src, dst, load_sem.at[len(loads)]))
        loads[-1].start()

    mine = pl.ds(2, ROWS)
    for p in range(3):
        load(cd_in.at[p], ga.at[mine, p])
    load(ca_in, ga.at[mine, 3])
    for p in range(2):
        load(co_in.at[p], ga.at[mine, 4 + p])
        load(el_in.at[p], ga.at[mine, 6 + p])
    for a in range(2):
        for p in range(3):
            load(ka_in.at[a, p], gb.at[mine, 3 * a + p])
    load(el_in.at[2], gb.at[mine, 6])
    load(el_in.at[2], gb.at[mine, 7])
    for k in range(LEVELS):
        load(h_in.at[k], h.at[mine, k])
        load(m_in.at[k], m.at[mine, k])
        load(v_in.at[:, k], v.at[:, mine, k])
        load(w_in.at[:, k], w.at[:, mine, k])
    for copy in loads:
        copy.wait()

    lane = lane_id()
    slot = lane & 7

    def field(f, row, t):
        if f < 3:
            return v[f, row, :, tile(t)]
        if f < 6:
            return w[f - 3, row, :, tile(t)]
        return (h, m, ga, gb)[f - 6][row, :, tile(t)]

    def strip(f, e):
        return jnp.where(lane >= 64, field(f, e, 1), field(f, e, 0))

    for b in range(3):
        rows = [r for r in range(FIRST[b], FIRST[b] + 16) if 0 <= r < ROWS]
        total = [jnp.zeros((LEVELS, LANES), F32)] * FIELDS
        for r in rows:
            q = (r - FIRST[b]) * 8
            mask = (lane >= q) & (lane < q + 4)
            for f in range(FIELDS):
                total[f] = jnp.where(mask, turn(strip(f, r + 2), q - 126), total[f])
        for f in range(FIELDS):
            own[f, b] = total[f]
        for s in range(2):
            pack = jnp.zeros((LEVELS, LANES), F32)
            for f in range(8 * s, min(8 * s + 8, FIELDS)):
                pack = jnp.where(slot == f - 8 * s, turn(total[f], f - 8 * s - 1), pack)
            to_right[b, s] = pack
        for s in range(3):
            pack = jnp.zeros((LEVELS, LANES), F32)
            for f in range(4 * s, min(4 * s + 4, FIELDS)):
                at = 2 * (f - 4 * s)
                pack = jnp.where((slot == at) | (slot == at + 1), turn(total[f], at - 2), pack)
            to_left[b, s] = pack

    pl.semaphore_wait(barrier, len(TARGETS))

    sends = []

    def send(src, dst, target):
        n = len(sends)
        sends.append(
            pltpu.make_async_remote_copy(
                src_ref=src, dst_ref=dst, send_sem=send_sem.at[n], recv_sem=recv_sem.at[n],
                device_id=device(*target), device_id_type=MESH,
            )
        )
        sends[-1].start()

    top, bottom = pl.ds(0, 2), pl.ds(EXT - 2, 2)
    last, lead = pl.ds(ROWS, 2), pl.ds(2, 2)
    for ref in (v, w):
        send(ref.at[0:2, last], ref.at[0:2, top], DOWN)
        send(ref.at[2, ROWS + 1], ref.at[2, 1], DOWN)
        send(ref.at[1:3, lead], ref.at[1:3, bottom], UP)
        send(ref.at[0, 2], ref.at[0, EXT - 2], UP)
    for ref in (h, m, ga, gb):
        send(ref.at[last], ref.at[top], DOWN)
        send(ref.at[lead], ref.at[bottom], UP)
    send(to_left.at[2], corner_tr, DOWN_LEFT)
    send(to_left.at[0], corner_br, UP_LEFT)
    send(to_right.at[0], corner_bl, UP_RIGHT)
    send(to_right, from_left, RIGHT)
    send(to_left, from_right, LEFT)

    def invert(row, _):
        for t in range(2):
            inverse[row, :, tile(t)] = 1.0 / ga[row, :, tile(t)]
        return 0

    lax.fori_loop(2, ROWS + 2, invert, 0)
    vertices(3, ROWS + 1, v, h, w, m, ga, gb, sums)
    energies(3, ROWS + 1, v, w, ga, gb, inverse, kin)
    cells(4, ROWS, sums, cell)

    for copy in sends:
        copy.wait()

    vertices(0, 3, v, h, w, m, ga, gb, sums)
    vertices(ROWS + 1, EXT, v, h, w, m, ga, gb, sums)
    energies(2, 3, v, w, ga, gb, inverse, kin)
    energies(ROWS + 1, ROWS + 2, v, w, ga, gb, inverse, kin)
    cells(1, 4, sums, cell)
    cells(ROWS, ROWS + 3, sums, cell)

    top_rows, bottom_rows = lane < 16, (lane >= 48) & (lane < 64)
    for b in range(3):
        right = [from_right[b, s] for s in range(3)]
        left = [from_left[b, s] for s in range(2)]
        if b == 0:
            right = [jnp.where(top_rows, turn(corner_tr[s], -32), right[s]) for s in range(3)]
        if b == 2:
            right = [jnp.where(bottom_rows, turn(corner_br[s], 32), right[s]) for s in range(3)]
            left = [jnp.where(bottom_rows, turn(corner_bl[s], 32), left[s]) for s in range(2)]
        for f in range(FIELDS):
            x = own[f, b]
            for r in ((-2, -1) if b == 0 else ((32, 33) if b == 2 else ())):
                q = (r - FIRST[b]) * 8
                x = jnp.where((lane >= q) & (lane < q + 4), turn(strip(f, r + 2), q - 126), x)
            y = turn(right[f // 4], 2 - 2 * (f % 4))
            z = turn(left[f // 8], 4 - f % 8)
            x = jnp.where(slot < 2, x, jnp.where(slot < 4, y, jnp.where(slot == 4, z, turn(x, 3))))
            rim[f, b] = x

    for b in range(3):

        def shift(x, di, dj):
            return turn(x, -(8 * di + dj))

        def geo(f, plane):
            return jnp.broadcast_to(rim[f, b, pl.ds(plane, 1), :], (LEVELS, LANES))

        vv, ww = [rim[k, b] for k in range(3)], [rim[3 + k, b] for k in range(3)]
        hh, mm = rim[6, b], rim[7, b]
        d = [geo(8, k) for k in range(3)]
        f = [vv[k] * d[k] for k in range(3)]
        g = [ww[k] * d[k] for k in range(3)]
        h_right, m_right = shift(hh, 0, 1), shift(mm, 0, 1)
        v0, w0 = first_vertex(
            geo(8, 4), geo(9, 0), geo(9, 1), geo(9, 2), f[0], f[1], shift(f[2], 1, 0), g[0], g[1], shift(g[2], 1, 0),
            hh, shift(hh, 1, 0), h_right, mm, shift(mm, 1, 0), m_right,
        )
        v1, w1 = second_vertex(
            geo(8, 5), geo(9, 3), geo(9, 4), geo(9, 5), f[1], f[2], shift(f[0], -1, 1), g[1], g[2], shift(g[0], -1, 1),
            hh, h_right, shift(hh, -1, 1), mm, m_right, shift(mm, -1, 1),
        )
        rim_v[0, b] = v0
        rim_v[1, b] = v1
        for n, (x0, x1) in enumerate(((v0, v1), (w0, w1))):
            here = x0 + x1
            rim_c[n, b] = (here + shift(x0, -1, 0) + shift(here + shift(x1, 1, 0), 0, -1)) * (1.0 / 6.0)
        length = (geo(8, 6), geo(8, 7), geo(9, 6))
        e = [energy_of(vv[k], ww[k], d[k], length[k]) for k in range(3)]
        rim_k[b] = (e[0] + e[1] + e[2] + shift(e[0], -1, 0) + shift(e[1] + shift(e[2], 1, 0), 0, -1)) / geo(8, 3)


def output_kernel(
    v, w, sums, cell, kin, inverse, rim_v, rim_c, rim_k,
    vertex_out, kinetic_out, cell_out, edge_out,
    vertex_buf, kinetic_buf, cell_buf, edge_buf, sem,
):
    lane = lane_id()
    is_last, is_first = lane == LANES - 1, lane == 0

    def pick(ref, n, row, s, to):
        block, q = rim_of(row)
        x = ref[block] if n is None else ref[n, block]
        return turn(x, to - (q + s))

    def cell_row(n, r):
        first, second = row_pair(cell, n, r + 2)
        if r >= 0 and r <= ROWS:
            first = jnp.where(is_first, pick(rim_c, n, r, 5, 0), first)
        second = jnp.where(is_last, pick(rim_c, n, r, 1, LANES - 1), second)
        return first, second

    def cell_right(n, r, pair):
        first, second = turn(pair[0], -1), turn(pair[1], -1)
        return jnp.where(is_last, second, first), jnp.where(is_last, pick(rim_c, n, r, 2, LANES - 1), second)

    def vertex_row(n, r):
        first, second = row_pair(sums, 2 * n, r + 2)
        return first, jnp.where(is_last, pick(rim_v, n, r, 1, LANES - 1), second)

    copies = []

    def put(src, dst):
        copies.append(pltpu.make_async_copy(src, dst, sem.at[len(copies)]))
        copies[-1].start()

    here = [cell_row(n, 0) for n in range(2)]
    upper_right = [cell_right(n, -1, cell_row(n, -1)) for n in range(2)]
    v0_above, v1 = vertex_row(0, -1), vertex_row(1, 0)
    for r in range(ROWS):
        lower = [cell_row(n, r + 1) for n in range(2)]
        right = [cell_right(n, r, here[n]) for n in range(2)]
        v0, v1_below = vertex_row(0, r), vertex_row(1, r + 1)
        first, second = turn(v1_below[0], 1), turn(v1_below[1], 1)
        v1_corner = (
            jnp.where(is_first, pick(rim_v, 1, r + 1, 4, 0), first),
            jnp.where(is_first, first, second),
        )
        energy = row_pair(kin, r)
        energy = (jnp.where(is_first, pick(rim_k, None, r, 5, 0), energy[0]), energy[1])
        velocity = [row_pair(v, k, r + 2) for k in range(3)]
        tendency = [row_pair(w, k, r + 2) for k in range(3)]
        factor = [spread_pair(inverse, r + 2, k) for k in range(3)]
        for t in range(2):
            vertex_buf[0, r, :, tile(t)] = v0[t]
            vertex_buf[1, r, :, tile(t)] = v1[t]
            kinetic_buf[r, :, tile(t)] = energy[t]
            cell_buf[r, :, tile(t)] = here[0][t]
            means = (v0[t] + v1_corner[t], v0[t] + v1[t], v1[t] + v0_above[t])
            sides = (lower, right, upper_right)
            for k in range(3):
                slope = velocity[k][t] * (sides[k][0][t] - here[0][t]) + tendency[k][t] * (sides[k][1][t] - here[1][t])
                edge_buf[k, r, :, tile(t)] = 0.5 * (means[k] - slope * factor[k][t])
        here, upper_right, v0_above, v1 = lower, right, v0, v1_below
        if r % 16 == 15:
            part = pl.ds(r - 15, 16)
            for k in range(LEVELS):
                put(vertex_buf.at[:, part, k], vertex_out.at[:, k, part])
                put(kinetic_buf.at[part, k], kinetic_out.at[k, part])
                put(cell_buf.at[part, k], cell_out.at[k, part])
                put(edge_buf.at[:, part, k], edge_out.at[:, k, part])
    for copy in copies:
        copy.wait()


def local(*args):
    args = [pltpu.with_memory_space_constraint(x, pltpu.HBM) for x in args]
    whole = pl.BlockSpec(memory_space=pltpu.VMEM)
    anywhere = pl.BlockSpec(memory_space=pl.ANY)
    wide = (LEVELS, 2 * LANES)
    thin = (LEVELS, LANES)
    passed = [
        (3, EXT, *wide), (3, EXT, *wide), (4, EXT, *wide), (2, EXT, *wide), (ROWS, *wide), (EXT, *wide),
        (2, 3, *thin), (2, 3, *thin), (3, *thin),
    ]
    grant = 24 << 20
    between = pl.pallas_call(
        exchange_kernel,
        out_shape=[pltpu.VMEM(s, F32) for s in passed],
        in_specs=[anywhere] * 9,
        out_specs=[whole] * len(passed),
        scratch_shapes=[
            pltpu.VMEM((EXT, *wide), F32), pltpu.VMEM((EXT, *wide), F32),
            pltpu.VMEM((EXT, *wide), F32), pltpu.VMEM((EXT, *wide), F32),
            pltpu.VMEM((FIELDS, 3, *thin), F32),
            pltpu.VMEM((3, 2, *thin), F32), pltpu.VMEM((3, 3, *thin), F32),
            pltpu.VMEM((3, 2, *thin), F32), pltpu.VMEM((3, 3, *thin), F32),
            pltpu.VMEM((3, *thin), F32), pltpu.VMEM((3, *thin), F32), pltpu.VMEM((2, *thin), F32),
            pltpu.VMEM((FIELDS, 3, *thin), F32),
            pltpu.SemaphoreType.DMA((48,)), pltpu.SemaphoreType.DMA((21,)), pltpu.SemaphoreType.DMA((21,)),
        ],
        compiler_params=pltpu.CompilerParams(collective_id=0, has_side_effects=True, vmem_limit_bytes=grant),
    )(*args)
    outs = [(2, LEVELS, ROWS, 2 * LANES), (LEVELS, ROWS, 2 * LANES), (LEVELS, ROWS, 2 * LANES), (3, LEVELS, ROWS, 2 * LANES)]
    return tuple(
        pl.pallas_call(
            output_kernel,
            out_shape=[jax.ShapeDtypeStruct(s, F32) for s in outs],
            in_specs=[whole] * len(passed),
            out_specs=[anywhere] * 4,
            scratch_shapes=[
                pltpu.VMEM((2, ROWS, *wide), F32), pltpu.VMEM((ROWS, *wide), F32),
                pltpu.VMEM((ROWS, *wide), F32), pltpu.VMEM((3, ROWS, *wide), F32),
                pltpu.SemaphoreType.DMA((64,)),
            ],
            compiler_params=pltpu.CompilerParams(vmem_limit_bytes=grant),
        )(*between)
    )


def solution(mesh):
    edges, cell = P(None, None, "py", "px"), P(None, "py", "px")
    return jax.shard_map(
        local,
        mesh=mesh,
        in_specs=(edges, cell, edges, cell, cell, cell, P("py", "px"), edges, cell),
        out_specs=(edges, cell, cell, edges),
        check_vma=False,
    )
```

time: 80.2 us -> 23.2 us (0.29)
  the two profiles are of different devices: /device:TPU:25 before, /device:TPU:0 now
where the time goes in v1:
time: 23.2 us; the launch traced here: 23 us
  Pallas kernels  22.4 us (97%)
  between operations  0.64 us (3%)
    pallas_call x1, Pallas kernels, local(): pl.pallas_call(exchange_kernel, out_shape=[pltpu.VMEM(s, F32) for s in pa...  18.5 us
    pallas_call x1, Pallas kernels, local(): pl.pallas_call(output_kernel, out_shape=[jax.ShapeDtypeStruct(s, F32) for...  3.87 us

profile of v1, /device:TPU:0, one launch (start us, length us, event | category | flops | bytes accessed | tf_op | source)
XLA Modules:
  0.0 23.0 jit_solution(12867816030184693664)
XLA Ops:
  0.6 18.5 %shard_map.120 = (f32[3,36,8,256]{3,2,1,0:T(8,128)S(1)}, f32[3,36,8,256]{3,2,1,0:T(8,128)S(1)}, f32[4,36,8,256]{3,2,1,0:T(8,128)S(1)}, f32[2,36,8,256]{3,2,1,0:T...) custom-call(f32[3,8,32,256]{3,2,1,0:T(8,128)} %v_in.1, ...), custom_call_target="tpu_custom_call" | custom-call | tf_op jit(solution)/shard_map/pallas_call | solution.py:442
  19.2 3.9 %shard_map.121 = (f32[2,8,32,256]{3,2,1,0:T(8,128)}, f32[8,32,256]{2,1,0:T(8,128)}, f32[8,32,256]{2,1,0:T(8,128)}, f32[3,8,32,256]{3,2,1,0:T(8,128)}) custom-call(f32[3,36,8,256]{3,2,1,0:T(8,128)S(1)} %get-tuple-element.13.v, f32[3,36,8,256]{3,2,1,0:T(8,128)S(1)} %get-tuple-element.14.w, f32[4,36,8,256]{3,2,1,0:T(8,128)S(1)} %get-tuple-element.15.sums, ...), custom_call_target="tpu_custom_call" | custom-call | tf_op jit(solution)/shard_map/pallas_call | solution.py:461

commit v2 on v1

v2 whole, which is shorter than its diff:
```python
import jax
import jax.numpy as jnp
from jax import lax
from jax.experimental import pallas as pl
from jax.experimental.pallas import tpu as pltpu
from jax.sharding import PartitionSpec as P

F32 = jnp.float32
MESH = pl.DeviceIdType.MESH
ROWS = 32
EXT = ROWS + 4
LEVELS = 8
LANES = 128

FIRST = (-2, 12, 26)
FIELDS = 10
GROUP = 6

DOWN, UP, RIGHT, LEFT = (1, 0), (-1, 0), (0, 1), (0, -1)
DOWN_LEFT, UP_LEFT, UP_RIGHT = (1, -1), (-1, -1), (-1, 1)
TARGETS = (DOWN, UP, RIGHT, LEFT, DOWN_LEFT, UP_LEFT, UP_RIGHT)


def rim_of(row):
    block = 0 if row <= 12 else (1 if row <= 26 else 2)
    return block, (row - FIRST[block]) * 8


def lane_id():
    return lax.broadcasted_iota(jnp.int32, (LEVELS, LANES), 1)


def turn(x, amount):
    amount = amount % LANES
    return x if amount == 0 else pltpu.roll(x, amount, 1)


def next_col(pair, lane):
    first, second = turn(pair[0], -1), turn(pair[1], -1)
    return jnp.where(lane == LANES - 1, second, first), second


def prev_col(pair, lane):
    first, second = turn(pair[0], 1), turn(pair[1], 1)
    return first, jnp.where(lane == 0, first, second)


def tile(t):
    return pl.ds(t * LANES, LANES)


def row_pair(ref, *index):
    return ref[(*index, slice(None), tile(0))], ref[(*index, slice(None), tile(1))]


def spread(ref, row, plane, t):
    return jnp.broadcast_to(ref[row, pl.ds(plane, 1), tile(t)], (LEVELS, LANES))


def spread_pair(ref, row, plane):
    return spread(ref, row, plane, 0), spread(ref, row, plane, 1)


def both(fn, *pairs):
    return tuple(fn(*(p[t] for p in pairs)) for t in range(2))


def add(a, b):
    return a + b


def mul(a, b):
    return a * b


def staged(rows, begin, finish, depth):
    waiting = []
    for row in rows:
        waiting.append((row, begin(row)))
        if len(waiting) > depth:
            finish(*waiting.pop(0))
    for row, value in waiting:
        finish(row, value)


def weigh(n0, n1, s0, s1):
    start = n0 / s0
    middle = (n0 + n0 + n1) / (s0 + s0 + s1)
    end = (n0 + n1) / (s0 + s1)
    twice = middle + middle
    late = twice + end
    return (start + twice + late) * (1.0 / 6.0), late * (1.0 / 6.0)


def first_vertex(cor, k0, k1, k2, f0, f1, f2_down, g0, g1, g2_down, h, h_down, h_right, m, m_down, m_right):
    n0 = cor * (k0 + k1 + k2) + (f0 + f2_down - f1)
    n1 = g0 + g2_down - g1
    s0 = k0 * h + k1 * h_down + k2 * h_right
    s1 = k0 * m + k1 * m_down + k2 * m_right
    return weigh(n0, n1, s0, s1)


def second_vertex(cor, k0, k1, k2, f1, f2, f0_diag, g1, g2, g0_diag, h, h_right, h_diag, m, m_right, m_diag):
    n0 = cor * (k0 + k1 + k2) + (f1 - f2 - f0_diag)
    n1 = g1 - g2 - g0_diag
    s0 = k0 * h + k1 * h_right + k2 * h_diag
    s1 = k0 * m + k1 * m_right + k2 * m_diag
    return weigh(n0, n1, s0, s1)


def energy_of(v, w, d, e):
    return (v * (v + w) + (w * w) * (1.0 / 3.0)) * (0.25 * d * e)


def turned_rows(rows, v, h, w, m, ga, right):
    def begin(row):
        d0 = spread_pair(ga, row, 0)
        pairs = (both(mul, row_pair(v, 0, row), d0), both(mul, row_pair(w, 0, row), d0), row_pair(h, row), row_pair(m, row))
        return [(turn(p[0], -1), turn(p[1], -1)) for p in pairs]

    def finish(row, turned):
        last = lane_id() == LANES - 1
        for n, (first, second) in enumerate(turned):
            right[n, row, :, tile(0)] = jnp.where(last, second, first)
            right[n, row, :, tile(1)] = second

    staged(rows, begin, finish, 8)


def vertex_rows(rows, v, h, w, m, ga, gb, right, out, depth=2, skip_first=None, skip_second=None):
    known = {}

    def flux(ref, name, k, row, key):
        if (name, k, key) not in known:
            known[name, k, key] = both(mul, row_pair(ref, k, row), spread_pair(ga, row, k))
        return known[name, k, key]

    def begin(item):
        key, row = item
        f = [flux(v, "v", k, row, key) for k in range(3)]
        g = [flux(w, "w", k, row, key) for k in range(3)]
        hh, mm = row_pair(h, row), row_pair(m, row)
        h_right, m_right = row_pair(right, 2, row), row_pair(right, 3, row)
        results = []
        if key != skip_first:
            below = row + 1
            f2_down, g2_down = flux(v, "v", 2, below, key + 1), flux(w, "w", 2, below, key + 1)
            h_down, m_down = row_pair(h, below), row_pair(m, below)
            cor = spread_pair(ga, row, 4)
            kite = [spread_pair(gb, row, p) for p in range(3)]
            for t in range(2):
                pair = first_vertex(
                    cor[t], kite[0][t], kite[1][t], kite[2][t], f[0][t], f[1][t], f2_down[t], g[0][t], g[1][t],
                    g2_down[t], hh[t], h_down[t], h_right[t], mm[t], m_down[t], m_right[t],
                )
                results += [(0, t, pair[0]), (1, t, pair[1])]
        if key != skip_second:
            above = row - 1
            f0_diag, g0_diag, h_diag, m_diag = (row_pair(right, n, above) for n in range(4))
            cor = spread_pair(ga, row, 5)
            kite = [spread_pair(gb, row, p) for p in range(3, 6)]
            for t in range(2):
                pair = second_vertex(
                    cor[t], kite[0][t], kite[1][t], kite[2][t], f[1][t], f[2][t], f0_diag[t], g[1][t], g[2][t],
                    g0_diag[t], hh[t], h_right[t], h_diag[t], mm[t], m_right[t], m_diag[t],
                )
                results += [(2, t, pair[0]), (3, t, pair[1])]
        return results

    def finish(item, results):
        for n, t, value in results:
            out[n, item[1], :, tile(t)] = value

    staged(rows, begin, finish, depth)


def cell_rows(rows, sums, out):
    def begin(row):
        values = []
        for n in range(2):
            v0, v1 = row_pair(sums, n, row), row_pair(sums, 2 + n, row)
            above, below = row_pair(sums, n, row - 1), row_pair(sums, 2 + n, row + 1)
            here = both(add, v0, v1)
            west = both(add, here, below)
            values.append((both(add, here, above), (turn(west[0], 1), turn(west[1], 1))))
        return values

    def finish(row, values):
        start = lane_id() == 0
        for n, (near, west) in enumerate(values):
            out[n, row, :, tile(0)] = (near[0] + west[0]) * (1.0 / 6.0)
            out[n, row, :, tile(1)] = (near[1] + jnp.where(start, west[0], west[1])) * (1.0 / 6.0)

    staged(rows, begin, finish, 5)


def energy_rows(rows, v, w, ga, gb, inverse, out):
    spots = ((ga, 6), (ga, 7), (gb, 6))
    known = {}

    def one(k, row):
        if (k, row) not in known:
            ref, plane = spots[k]
            known[k, row] = both(
                energy_of, row_pair(v, k, row), row_pair(w, k, row), spread_pair(ga, row, k), spread_pair(ref, row, plane)
            )
        return known[k, row]

    def begin(row):
        e1 = one(1, row)
        near = both(lambda a, b, c, d: a + b + (c + d), one(0, row), one(0, row - 1), e1, one(2, row))
        west = both(add, e1, one(2, row + 1))
        return near, (turn(west[0], 1), turn(west[1], 1))

    def finish(row, values):
        near, west = values
        start = lane_id() == 0
        area = spread_pair(inverse, row, 3)
        out[row - 2, :, tile(0)] = (near[0] + west[0]) * area[0]
        out[row - 2, :, tile(1)] = (near[1] + jnp.where(start, west[0], west[1])) * area[1]

    staged(rows, begin, finish, 6)


def exchange_kernel(
    v_in, h_in, w_in, m_in, cd_in, el_in, ca_in, ka_in, co_in,
    v, w, sums, cell, kin, inverse, rim_patch, rim_c, rim_right,
    h, m, ga, gb, turned, own, to_right, to_left, from_left, from_right, corner_tr, corner_br, corner_bl, rim,
    load_sem, send_sem, recv_sem,
):
    ny, nx = lax.axis_size("py"), lax.axis_size("px")
    my, mx = lax.axis_index("py"), lax.axis_index("px")

    def device(dy, dx):
        return {"py": lax.rem(my + dy + ny, ny), "px": lax.rem(mx + dx + nx, nx)}

    barrier = pltpu.get_barrier_semaphore()
    for dy, dx in TARGETS:
        pl.semaphore_signal(barrier, inc=1, device_id=device(-dy, -dx), device_id_type=MESH)

    loads = []

    def load(src, dst):
        loads.append(pltpu.make_async_copy(src, dst, load_sem.at[len(loads)]))
        loads[-1].start()

    mine = pl.ds(2, ROWS)
    for k in range(LEVELS):
        load(v_in.at[:, k], v.at[:, mine, k])
        load(w_in.at[:, k], w.at[:, mine, k])
        load(h_in.at[k], h.at[mine, k])
        load(m_in.at[k], m.at[mine, k])
    for p in range(3):
        load(cd_in.at[p], ga.at[mine, p])
    load(ca_in, ga.at[mine, 3])
    for p in range(2):
        load(co_in.at[p], ga.at[mine, 4 + p])
        load(el_in.at[p], ga.at[mine, 6 + p])
    for a in range(2):
        for p in range(3):
            load(ka_in.at[a, p], gb.at[mine, 3 * a + p])
    load(el_in.at[2], gb.at[mine, 6])
    load(el_in.at[2], gb.at[mine, 7])
    for copy in loads:
        copy.wait()

    lane = lane_id()
    slot = lane & 7

    def field(f, row, t):
        if f < 3:
            return v[f, row, :, tile(t)]
        if f < 6:
            return w[f - 3, row, :, tile(t)]
        return (h, m, ga, gb)[f - 6][row, :, tile(t)]

    def strip(f, e):
        return jnp.where(lane >= 64, field(f, e, 1), field(f, e, 0))

    total = {}
    for b in range(3):
        rows = [r for r in range(FIRST[b], FIRST[b] + 16) if 0 <= r < ROWS]
        masks = [(lane >= (r - FIRST[b]) * 8) & (lane < (r - FIRST[b]) * 8 + 4) for r in rows]
        for f in range(FIELDS):
            x = jnp.zeros((LEVELS, LANES), F32)
            for r, mask in zip(rows, masks):
                x = jnp.where(mask, turn(strip(f, r + 2), (r - FIRST[b]) * 8 - 126), x)
            total[f, b] = x
    packs = {}
    for b in range(3):
        for s in range(2):
            x = jnp.zeros((LEVELS, LANES), F32)
            for f in range(8 * s, min(8 * s + 8, FIELDS)):
                x = jnp.where(slot == f - 8 * s, turn(total[f, b], f - 8 * s - 1), x)
            packs[0, b, s] = x
        for s in range(3):
            x = jnp.zeros((LEVELS, LANES), F32)
            for f in range(4 * s, min(4 * s + 4, FIELDS)):
                at = 2 * (f - 4 * s)
                x = jnp.where((slot >> 1) == f - 4 * s, turn(total[f, b], at - 2), x)
            packs[1, b, s] = x
    for (n, b, s), x in packs.items():
        (to_right, to_left)[n][b, s] = x
    for (f, b), x in total.items():
        own[f, b] = x

    pl.semaphore_wait(barrier, len(TARGETS))

    sends = []

    def send(src, dst, target):
        n = len(sends)
        sends.append(
            pltpu.make_async_remote_copy(
                src_ref=src, dst_ref=dst, send_sem=send_sem.at[n], recv_sem=recv_sem.at[n],
                device_id=device(*target), device_id_type=MESH,
            )
        )
        sends[-1].start()

    top, bottom = pl.ds(0, 2), pl.ds(EXT - 2, 2)
    last, lead = pl.ds(ROWS, 2), pl.ds(2, 2)
    for ref in (v, w):
        send(ref.at[0:2, last], ref.at[0:2, top], DOWN)
        send(ref.at[2, ROWS + 1], ref.at[2, 1], DOWN)
        send(ref.at[1:3, lead], ref.at[1:3, bottom], UP)
        send(ref.at[0, 2], ref.at[0, EXT - 2], UP)
    for ref in (h, m, ga, gb):
        send(ref.at[last], ref.at[top], DOWN)
        send(ref.at[lead], ref.at[bottom], UP)
    send(to_left.at[2], corner_tr, DOWN_LEFT)
    send(to_left.at[0], corner_br, UP_LEFT)
    send(to_right.at[0], corner_bl, UP_RIGHT)
    send(to_right, from_left, RIGHT)
    send(to_left, from_right, LEFT)

    def invert(row):
        return [1.0 / ga[row, :, tile(t)] for t in range(2)]

    def keep(row, values):
        for t in range(2):
            inverse[row, :, tile(t)] = values[t]

    staged(range(2, ROWS + 2), invert, keep, 8)
    turned_rows(range(2, ROWS + 2), v, h, w, m, ga, turned)
    energy_rows(range(3, ROWS + 1), v, w, ga, gb, inverse, kin)

    def group(index, _):
        base = 3 + index * GROUP
        vertex_rows([(j, base + j) for j in range(GROUP)], v, h, w, m, ga, gb, turned, sums)
        return 0

    lax.fori_loop(0, (ROWS - 2) // GROUP, group, 0)
    cell_rows(range(4, ROWS), sums, cell)

    for copy in sends:
        copy.wait()

    top_rows, bottom_rows = lane < 16, (lane >= 48) & (lane < 64)
    strips = {}
    for b in range(3):
        right = [from_right[b, s] for s in range(3)]
        left = [from_left[b, s] for s in range(2)]
        if b == 0:
            right = [jnp.where(top_rows, turn(corner_tr[s], -32), right[s]) for s in range(3)]
        if b == 2:
            right = [jnp.where(bottom_rows, turn(corner_br[s], 32), right[s]) for s in range(3)]
            left = [jnp.where(bottom_rows, turn(corner_bl[s], 32), left[s]) for s in range(2)]
        for f in range(FIELDS):
            x = own[f, b]
            for r in ((-2, -1) if b == 0 else ((32, 33) if b == 2 else ())):
                q = (r - FIRST[b]) * 8
                x = jnp.where((lane >= q) & (lane < q + 4), turn(strip(f, r + 2), q - 126), x)
            y = turn(right[f // 4], 2 - 2 * (f % 4))
            z = turn(left[f // 8], 4 - f % 8)
            strips[f, b] = jnp.where(slot < 2, x, jnp.where(slot < 4, y, jnp.where(slot == 4, z, turn(x, 3))))
    turned_rows((0, 1, EXT - 2, EXT - 1), v, h, w, m, ga, turned)
    for (f, b), x in strips.items():
        rim[f, b] = x

    results = {}

    def shift(x, di, dj):
        return turn(x, -(8 * di + dj))

    for b in range(3):

        def geo(f, plane):
            return jnp.broadcast_to(rim[f, b, pl.ds(plane, 1), :], (LEVELS, LANES))

        vv, ww = [rim[k, b] for k in range(3)], [rim[3 + k, b] for k in range(3)]
        hh, mm = rim[6, b], rim[7, b]
        d = [geo(8, k) for k in range(3)]
        f = [vv[k] * d[k] for k in range(3)]
        g = [ww[k] * d[k] for k in range(3)]
        h_right, m_right = shift(hh, 0, 1), shift(mm, 0, 1)
        v0, w0 = first_vertex(
            geo(8, 4), geo(9, 0), geo(9, 1), geo(9, 2), f[0], f[1], shift(f[2], 1, 0), g[0], g[1], shift(g[2], 1, 0),
            hh, shift(hh, 1, 0), h_right, mm, shift(mm, 1, 0), m_right,
        )
        v1, w1 = second_vertex(
            geo(8, 5), geo(9, 3), geo(9, 4), geo(9, 5), f[1], f[2], shift(f[0], -1, 1), g[1], g[2], shift(g[0], -1, 1),
            hh, h_right, shift(hh, -1, 1), mm, m_right, shift(mm, -1, 1),
        )
        length = (geo(8, 6), geo(8, 7), geo(9, 6))
        e = [energy_of(vv[k], ww[k], d[k], length[k]) for k in range(3)]
        energy = (e[0] + e[1] + e[2] + shift(e[0], -1, 0) + (shift(e[1], 0, -1) + shift(e[2], 1, -1))) / geo(8, 3)
        results[0, 0, b] = jnp.where(slot == 0, shift(v0, 0, 1), shift(energy, 0, 4))
        results[0, 1, b] = jnp.where(slot == 0, shift(v1, 0, 1), shift(v1, 1, 3))
        for n, (x0, x1) in enumerate(((v0, v1), (w0, w1))):
            here = x0 + x1
            mean = (here + shift(x0, -1, 0) + (shift(here, 0, -1) + shift(x1, 1, -1))) * (1.0 / 6.0)
            results[1, n, b] = jnp.where(slot == 0, shift(mean, 0, 1), shift(mean, 0, 4))
            results[2, n, b] = mean
    for (which, n, b), x in results.items():
        (rim_patch, rim_c, rim_right)[which][n, b] = x

    vertex_rows([(e, e) for e in (0, 1, 2, ROWS + 1, ROWS + 2, ROWS + 3)], v, h, w, m, ga, gb, turned, sums, 2, EXT - 1, 0)
    energy_rows((2, ROWS + 1), v, w, ga, gb, inverse, kin)
    cell_rows((1, 2, 3, ROWS, ROWS + 1, ROWS + 2), sums, cell)


def output_kernel(
    v, w, sums, cell, kin, inverse, rim_patch, rim_c, rim_right,
    vertex_out, kinetic_out, cell_out, edge_out,
    vertex_buf, kinetic_buf, cell_buf, edge_buf, other_buf, right_buf, corner_buf, sem,
):
    lane = lane_id()
    is_last, is_first, tail = lane == LANES - 1, lane == 0, lane >= LANES - 2

    def pick(ref, n, row, s, to):
        block, q = rim_of(row)
        return turn(ref[n, block], to - (q + s))

    copies = []

    def put(src, dst):
        copies.append(pltpu.make_async_copy(src, dst, sem.at[len(copies)]))
        copies[-1].start()

    def begin(r):
        values = []
        for n in range(2):
            pair = row_pair(cell, n, r + 2)
            values += [pair, turn(pair[0], -1), turn(pair[1], -1), pick(rim_c, n, r, 0, LANES - 1), pick(rim_right, n, r, 1, LANES - 2)]
        if r < ROWS:
            values += [row_pair(sums, 0, r + 2), pick(rim_patch, 0, r, 0, LANES - 1)]
            if r >= 0:
                values += [row_pair(sums, 2, r + 2), row_pair(kin, r), pick(rim_patch, 1, r, 0, LANES - 1)]
                below = row_pair(sums, 2, r + 3)
                values += [turn(below[0], 1), turn(below[1], 1)]
        return values

    def finish(r, values):
        for n, buf in ((0, cell_buf), (1, other_buf)):
            pair, first, second, patch, patch_right = values[5 * n : 5 * n + 5]
            buf[r + 1, :, tile(0)] = jnp.where(is_first, patch, pair[0])
            buf[r + 1, :, tile(1)] = jnp.where(is_last, patch, pair[1])
            right_buf[n, r + 1, :, tile(0)] = jnp.where(is_last, second, first)
            right_buf[n, r + 1, :, tile(1)] = jnp.where(tail, patch_right, second)
        if r < ROWS:
            v0, patch = values[10:12]
            vertex_buf[0, r + 1, :, tile(0)] = v0[0]
            vertex_buf[0, r + 1, :, tile(1)] = jnp.where(is_last, patch, v0[1])
            if r >= 0:
                v1, energy, other, first, second = values[12:17]
                kinetic_buf[r, :, tile(0)] = jnp.where(is_first, patch, energy[0])
                kinetic_buf[r, :, tile(1)] = energy[1]
                vertex_buf[1, r + 1, :, tile(0)] = v1[0]
                vertex_buf[1, r + 1, :, tile(1)] = jnp.where(is_last, other, v1[1])
                corner_buf[r, :, tile(0)] = jnp.where(is_first, other, first)
                corner_buf[r, :, tile(1)] = jnp.where(is_first, first, second)

    staged(range(-1, ROWS + 1), begin, finish, 8)
    for k in range(LEVELS):
        put(vertex_buf.at[:, 1 : ROWS + 1, k], vertex_out.at[:, k])
        put(kinetic_buf.at[:, k], kinetic_out.at[k])
        put(cell_buf.at[1 : ROWS + 1, k], cell_out.at[k])

    def slopes(r):
        v0, v1 = row_pair(vertex_buf, 0, r + 1), row_pair(vertex_buf, 1, r + 1)
        means = (
            both(add, v0, row_pair(corner_buf, r)),
            both(add, v0, v1),
            both(add, v1, row_pair(vertex_buf, 0, r)),
        )
        here = (row_pair(cell_buf, r + 1), row_pair(other_buf, r + 1))
        lower = (row_pair(cell_buf, r + 2), row_pair(other_buf, r + 2))
        right = (row_pair(right_buf, 0, r + 1), row_pair(right_buf, 1, r + 1))
        upper = (row_pair(right_buf, 0, r), row_pair(right_buf, 1, r))
        values = []
        for k, side in enumerate((lower, right, upper)):
            velocity, tendency = row_pair(v, k, r + 2), row_pair(w, k, r + 2)
            factor = spread_pair(inverse, r + 2, k)
            for t in range(2):
                slope = velocity[t] * (side[0][t] - here[0][t]) + tendency[t] * (side[1][t] - here[1][t])
                values.append(0.5 * (means[k][t] - slope * factor[t]))
        return values

    def keep(r, values):
        for k in range(3):
            for t in range(2):
                edge_buf[k, r, :, tile(t)] = values[2 * k + t]

    half = ROWS // 2
    for part in range(2):
        rows = pl.ds(part * half, half)
        staged(range(part * half, (part + 1) * half), slopes, keep, 3)
        for k in range(LEVELS):
            put(edge_buf.at[:, rows, k], edge_out.at[:, k, rows])
    for copy in copies:
        copy.wait()


def local(*args):
    args = [pltpu.with_memory_space_constraint(x, pltpu.HBM) for x in args]
    whole = pl.BlockSpec(memory_space=pltpu.VMEM)
    anywhere = pl.BlockSpec(memory_space=pl.ANY)
    wide = (LEVELS, 2 * LANES)
    thin = (LEVELS, LANES)
    passed = [
        (3, EXT, *wide), (3, EXT, *wide), (4, EXT, *wide), (2, EXT, *wide), (ROWS, *wide), (EXT, *wide),
        (2, 3, *thin), (2, 3, *thin), (2, 3, *thin),
    ]
    grant = 24 << 20
    between = pl.pallas_call(
        exchange_kernel,
        out_shape=[pltpu.VMEM(s, F32) for s in passed],
        in_specs=[anywhere] * 9,
        out_specs=[whole] * len(passed),
        scratch_shapes=[
            pltpu.VMEM((EXT, *wide), F32), pltpu.VMEM((EXT, *wide), F32),
            pltpu.VMEM((EXT, *wide), F32), pltpu.VMEM((EXT, *wide), F32),
            pltpu.VMEM((4, EXT, *wide), F32), pltpu.VMEM((FIELDS, 3, *thin), F32),
            pltpu.VMEM((3, 2, *thin), F32), pltpu.VMEM((3, 3, *thin), F32),
            pltpu.VMEM((3, 2, *thin), F32), pltpu.VMEM((3, 3, *thin), F32),
            pltpu.VMEM((3, *thin), F32), pltpu.VMEM((3, *thin), F32), pltpu.VMEM((2, *thin), F32),
            pltpu.VMEM((FIELDS, 3, *thin), F32),
            pltpu.SemaphoreType.DMA((48,)), pltpu.SemaphoreType.DMA((21,)), pltpu.SemaphoreType.DMA((21,)),
        ],
        compiler_params=pltpu.CompilerParams(collective_id=0, has_side_effects=True, vmem_limit_bytes=grant),
    )(*args)
    outs = [(2, LEVELS, ROWS, 2 * LANES), (LEVELS, ROWS, 2 * LANES), (LEVELS, ROWS, 2 * LANES), (3, LEVELS, ROWS, 2 * LANES)]
    return tuple(
        pl.pallas_call(
            output_kernel,
            out_shape=[jax.ShapeDtypeStruct(s, F32) for s in outs],
            in_specs=[whole] * len(passed),
            out_specs=[anywhere] * 4,
            scratch_shapes=[
                pltpu.VMEM((2, ROWS + 1, *wide), F32), pltpu.VMEM((ROWS, *wide), F32),
                pltpu.VMEM((ROWS + 2, *wide), F32), pltpu.VMEM((3, ROWS, *wide), F32),
                pltpu.VMEM((ROWS + 2, *wide), F32), pltpu.VMEM((2, ROWS + 2, *wide), F32), pltpu.VMEM((ROWS, *wide), F32),
                pltpu.SemaphoreType.DMA((64,)),
            ],
            compiler_params=pltpu.CompilerParams(vmem_limit_bytes=grant),
        )(*between)
    )


def solution(mesh):
    edges, cell = P(None, None, "py", "px"), P(None, "py", "px")
    return jax.shard_map(
        local,
        mesh=mesh,
        in_specs=(edges, cell, edges, cell, cell, cell, P("py", "px"), edges, cell),
        out_specs=(edges, cell, cell, edges),
        check_vma=False,
    )
```

time: 23.2 us -> 17.5 us (0.75)
  Pallas kernels: 22.4 us -> 16.7 us
    pallas_call x1, Pallas kernels: 18.5 us -> 14.5 us  [local(): pl.pallas_call(exchange_kernel, out_shape=[pltpu.VMEM(s, F32) for s in pa...]
    pallas_call x1, Pallas kernels: 3.87 us -> 2.2 us  [local(): pl.pallas_call(output_kernel, out_shape=[jax.ShapeDtypeStruct(s, F32) for...]
where the time goes in v2:
time: 17.5 us; the launch traced here: 17.4 us
  Pallas kernels  16.7 us (95%)
  between operations  0.64 us (4%)
    pallas_call x1, Pallas kernels, local(): pl.pallas_call(exchange_kernel, out_shape=[pltpu.VMEM(s, F32) for s in pa...  14.5 us
    pallas_call x1, Pallas kernels, local(): pl.pallas_call(output_kernel, out_shape=[jax.ShapeDtypeStruct(s, F32) for...  2.2 us

profile of v2, /device:TPU:0, one launch (start us, length us, event | category | flops | bytes accessed | tf_op | source)
XLA Modules:
  0.0 17.4 jit_solution(9239317744828626580)
XLA Ops:
  0.6 14.5 %shard_map.120 = (f32[3,36,8,256]{3,2,1,0:T(8,128)S(1)}, f32[3,36,8,256]{3,2,1,0:T(8,128)S(1)}, f32[4,36,8,256]{3,2,1,0:T(8,128)S(1)}, f32[2,36,8,256]{3,2,1,0:T...) custom-call(f32[3,8,32,256]{3,2,1,0:T(8,128)} %v_in.1, ...), custom_call_target="tpu_custom_call" | custom-call | tf_op jit(solution)/shard_map/pallas_call | solution.py:526
  15.2 2.2 %shard_map.121 = (f32[2,8,32,256]{3,2,1,0:T(8,128)}, f32[8,32,256]{2,1,0:T(8,128)}, f32[8,32,256]{2,1,0:T(8,128)}, f32[3,8,32,256]{3,2,1,0:T(8,128)}) custom-call(f32[3,36,8,256]{3,2,1,0:T(8,128)S(1)} %get-tuple-element.13.v, f32[3,36,8,256]{3,2,1,0:T(8,128)S(1)} %get-tuple-element.14.w, f32[4,36,8,256]{3,2,1,0:T(8,128)S(1)} %get-tuple-element.15.sums, ...), custom_call_target="tpu_custom_call" | custom-call | tf_op jit(solution)/shard_map/pallas_call | solution.py:545

commit v3 on v2

--- a/solution.py
+++ b/solution.py
@@ -18,7 +18,7 @@
 
 DOWN, UP, RIGHT, LEFT = (1, 0), (-1, 0), (0, 1), (0, -1)
 DOWN_LEFT, UP_LEFT, UP_RIGHT = (1, -1), (-1, -1), (-1, 1)
-TARGETS = (DOWN, UP, RIGHT, LEFT, DOWN_LEFT, UP_LEFT, UP_RIGHT)
+TARGETS = (DOWN, UP, RIGHT, LEFT, DOWN_LEFT, UP_RIGHT)
 
 
 def rim_of(row):
@@ -226,7 +226,7 @@
     v_in, h_in, w_in, m_in, cd_in, el_in, ca_in, ka_in, co_in,
     v, w, sums, cell, kin, inverse, rim_patch, rim_c, rim_right,
     h, m, ga, gb, turned, own, to_right, to_left, from_left, from_right, corner_tr, corner_br, corner_bl, rim,
-    load_sem, send_sem, recv_sem,
+    load_sem, send_sem, recv_sem, corner_sem,
 ):
     ny, nx = lax.axis_size("py"), lax.axis_size("px")
     my, mx = lax.axis_index("py"), lax.axis_index("px")
@@ -305,6 +305,7 @@
         own[f, b] = x
 
     pl.semaphore_wait(barrier, len(TARGETS))
+    pl.semaphore_signal(corner_sem, inc=1, device_id=device(*RIGHT), device_id_type=MESH)
 
     sends = []
 
@@ -329,7 +330,6 @@
         send(ref.at[last], ref.at[top], DOWN)
         send(ref.at[lead], ref.at[bottom], UP)
     send(to_left.at[2], corner_tr, DOWN_LEFT)
-    send(to_left.at[0], corner_br, UP_LEFT)
     send(to_right.at[0], corner_bl, UP_RIGHT)
     send(to_right, from_left, RIGHT)
     send(to_left, from_right, LEFT)
@@ -343,6 +343,8 @@
 
     staged(range(2, ROWS + 2), invert, keep, 8)
     turned_rows(range(2, ROWS + 2), v, h, w, m, ga, turned)
+    pl.semaphore_wait(corner_sem, 1)
+    send(to_left.at[0], corner_br, UP_LEFT)
     energy_rows(range(3, ROWS + 1), v, w, ga, gb, inverse, kin)
 
     def group(index, _):
@@ -354,7 +356,7 @@
     cell_rows(range(4, ROWS), sums, cell)
 
     for copy in sends:
-        copy.wait()
+        copy.wait_recv()
 
     top_rows, bottom_rows = lane < 16, (lane >= 48) & (lane < 64)
     strips = {}
@@ -418,6 +420,8 @@
     vertex_rows([(e, e) for e in (0, 1, 2, ROWS + 1, ROWS + 2, ROWS + 3)], v, h, w, m, ga, gb, turned, sums, 2, EXT - 1, 0)
     energy_rows((2, ROWS + 1), v, w, ga, gb, inverse, kin)
     cell_rows((1, 2, 3, ROWS, ROWS + 1, ROWS + 2), sums, cell)
+    for copy in sends:
+        copy.wait_send()
 
 
 def output_kernel(
@@ -537,6 +541,7 @@
             pltpu.VMEM((3, *thin), F32), pltpu.VMEM((3, *thin), F32), pltpu.VMEM((2, *thin), F32),
             pltpu.VMEM((FIELDS, 3, *thin), F32),
             pltpu.SemaphoreType.DMA((48,)), pltpu.SemaphoreType.DMA((21,)), pltpu.SemaphoreType.DMA((21,)),
+            pltpu.SemaphoreType.REGULAR,
         ],
         compiler_params=pltpu.CompilerParams(collective_id=0, has_side_effects=True, vmem_limit_bytes=grant),
     )(*args)

time: 17.5 us -> 17.1 us (0.977)
  Pallas kernels: 16.7 us -> 16.3 us
    pallas_call x1, Pallas kernels: 14.5 us -> 14.1 us  [local(): pl.pallas_call(exchange_kernel, out_shape=[pltpu.VMEM(s, F32) for s in pa...]
where the time goes in v3:
time: 17.1 us; the launch traced here: 17 us
  Pallas kernels  16.3 us (95%)
  between operations  0.64 us (4%)
    pallas_call x1, Pallas kernels, local(): pl.pallas_call(exchange_kernel, out_shape=[pltpu.VMEM(s, F32) for s in pa...  14.1 us
    pallas_call x1, Pallas kernels, local(): pl.pallas_call(output_kernel, out_shape=[jax.ShapeDtypeStruct(s, F32) for...  2.2 us

profile of v3, /device:TPU:0, one launch (start us, length us, event | category | flops | bytes accessed | tf_op | source)
XLA Modules:
  0.0 17.0 jit_solution(7961937276431368692)
XLA Ops:
  0.6 14.1 %shard_map.120 = (f32[3,36,8,256]{3,2,1,0:T(8,128)S(1)}, f32[3,36,8,256]{3,2,1,0:T(8,128)S(1)}, f32[4,36,8,256]{3,2,1,0:T(8,128)S(1)}, f32[2,36,8,256]{3,2,1,0:T...) custom-call(f32[3,8,32,256]{3,2,1,0:T(8,128)} %v_in.1, ...), custom_call_target="tpu_custom_call" | custom-call | tf_op jit(solution)/shard_map/pallas_call | solution.py:530
  14.8 2.2 %shard_map.121 = (f32[2,8,32,256]{3,2,1,0:T(8,128)}, f32[8,32,256]{2,1,0:T(8,128)}, f32[8,32,256]{2,1,0:T(8,128)}, f32[3,8,32,256]{3,2,1,0:T(8,128)}) custom-call(f32[3,36,8,256]{3,2,1,0:T(8,128)S(1)} %get-tuple-element.13.v, f32[3,36,8,256]{3,2,1,0:T(8,128)S(1)} %get-tuple-element.14.w, f32[4,36,8,256]{3,2,1,0:T(8,128)S(1)} %get-tuple-element.15.sums, ...), custom_call_target="tpu_custom_call" | custom-call | tf_op jit(solution)/shard_map/pallas_call | solution.py:550

commit v4 on v3

--- a/solution.py
+++ b/solution.py
@@ -18,7 +18,6 @@
 
 DOWN, UP, RIGHT, LEFT = (1, 0), (-1, 0), (0, 1), (0, -1)
 DOWN_LEFT, UP_LEFT, UP_RIGHT = (1, -1), (-1, -1), (-1, 1)
-TARGETS = (DOWN, UP, RIGHT, LEFT, DOWN_LEFT, UP_RIGHT)
 
 
 def rim_of(row):
@@ -226,7 +225,7 @@
     v_in, h_in, w_in, m_in, cd_in, el_in, ca_in, ka_in, co_in,
     v, w, sums, cell, kin, inverse, rim_patch, rim_c, rim_right,
     h, m, ga, gb, turned, own, to_right, to_left, from_left, from_right, corner_tr, corner_br, corner_bl, rim,
-    load_sem, send_sem, recv_sem, corner_sem,
+    load_sem, send_sem, recv_sem, left_sem,
 ):
     ny, nx = lax.axis_size("py"), lax.axis_size("px")
     my, mx = lax.axis_index("py"), lax.axis_index("px")
@@ -235,8 +234,12 @@
         return {"py": lax.rem(my + dy + ny, ny), "px": lax.rem(mx + dx + nx, nx)}
 
     barrier = pltpu.get_barrier_semaphore()
-    for dy, dx in TARGETS:
-        pl.semaphore_signal(barrier, inc=1, device_id=device(-dy, -dx), device_id_type=MESH)
+
+    def tell(sem, target):
+        pl.semaphore_signal(sem, inc=1, device_id=device(*target), device_id_type=MESH)
+
+    for target in (DOWN, UP, LEFT, DOWN_LEFT):
+        tell(barrier, target)
 
     loads = []
 
@@ -245,11 +248,6 @@
         loads[-1].start()
 
     mine = pl.ds(2, ROWS)
-    for k in range(LEVELS):
-        load(v_in.at[:, k], v.at[:, mine, k])
-        load(w_in.at[:, k], w.at[:, mine, k])
-        load(h_in.at[k], h.at[mine, k])
-        load(m_in.at[k], m.at[mine, k])
     for p in range(3):
         load(cd_in.at[p], ga.at[mine, p])
     load(ca_in, ga.at[mine, 3])
@@ -261,8 +259,19 @@
             load(ka_in.at[a, p], gb.at[mine, 3 * a + p])
     load(el_in.at[2], gb.at[mine, 6])
     load(el_in.at[2], gb.at[mine, 7])
-    for copy in loads:
-        copy.wait()
+    steps = [len(loads)]
+    for src, dst in ((h_in, h), (m_in, m)):
+        for k in range(LEVELS):
+            load(src.at[k], dst.at[mine, k])
+    steps.append(len(loads))
+    for src, dst in ((v_in, v), (w_in, w)):
+        for k in range(LEVELS):
+            load(src.at[:, k], dst.at[:, mine, k])
+        steps.append(len(loads))
+
+    def arrived(step):
+        for copy in loads[steps[step - 1] if step else 0 : steps[step]]:
+            copy.wait()
 
     lane = lane_id()
     slot = lane & 7
@@ -278,34 +287,36 @@
         return jnp.where(lane >= 64, field(f, e, 1), field(f, e, 0))
 
     total = {}
-    for b in range(3):
-        rows = [r for r in range(FIRST[b], FIRST[b] + 16) if 0 <= r < ROWS]
-        masks = [(lane >= (r - FIRST[b]) * 8) & (lane < (r - FIRST[b]) * 8 + 4) for r in rows]
-        for f in range(FIELDS):
-            x = jnp.zeros((LEVELS, LANES), F32)
-            for r, mask in zip(rows, masks):
-                x = jnp.where(mask, turn(strip(f, r + 2), (r - FIRST[b]) * 8 - 126), x)
-            total[f, b] = x
+    for step, fields in enumerate(((8, 9), (6, 7), (0, 1, 2), (3, 4, 5))):
+        arrived(step)
+        for b in (2, 0, 1):
+            rows = [r for r in range(FIRST[b], FIRST[b] + 16) if 0 <= r < ROWS]
+            masks = [(lane >= (r - FIRST[b]) * 8) & (lane < (r - FIRST[b]) * 8 + 4) for r in rows]
+            for f in fields:
+                x = jnp.zeros((LEVELS, LANES), F32)
+                for r, mask in zip(rows, masks):
+                    x = jnp.where(mask, turn(strip(f, r + 2), (r - FIRST[b]) * 8 - 126), x)
+                total[f, b] = x
     packs = {}
-    for b in range(3):
-        for s in range(2):
-            x = jnp.zeros((LEVELS, LANES), F32)
-            for f in range(8 * s, min(8 * s + 8, FIELDS)):
-                x = jnp.where(slot == f - 8 * s, turn(total[f, b], f - 8 * s - 1), x)
-            packs[0, b, s] = x
+    for b in (2, 0, 1):
         for s in range(3):
             x = jnp.zeros((LEVELS, LANES), F32)
             for f in range(4 * s, min(4 * s + 4, FIELDS)):
                 at = 2 * (f - 4 * s)
                 x = jnp.where((slot >> 1) == f - 4 * s, turn(total[f, b], at - 2), x)
             packs[1, b, s] = x
+        for s in range(2):
+            x = jnp.zeros((LEVELS, LANES), F32)
+            for f in range(8 * s, min(8 * s + 8, FIELDS)):
+                x = jnp.where(slot == f - 8 * s, turn(total[f, b], f - 8 * s - 1), x)
+            packs[0, b, s] = x
     for (n, b, s), x in packs.items():
         (to_right, to_left)[n][b, s] = x
     for (f, b), x in total.items():
         own[f, b] = x
 
-    pl.semaphore_wait(barrier, len(TARGETS))
-    pl.semaphore_signal(corner_sem, inc=1, device_id=device(*RIGHT), device_id_type=MESH)
+    pl.semaphore_wait(barrier, 4)
+    tell(left_sem, RIGHT)
 
     sends = []
 
@@ -318,21 +329,21 @@
             )
         )
         sends[-1].start()
+        return sends[-1]
 
     top, bottom = pl.ds(0, 2), pl.ds(EXT - 2, 2)
     last, lead = pl.ds(ROWS, 2), pl.ds(2, 2)
+    row_sends, rim_sends = [], []
     for ref in (v, w):
-        send(ref.at[0:2, last], ref.at[0:2, top], DOWN)
-        send(ref.at[2, ROWS + 1], ref.at[2, 1], DOWN)
-        send(ref.at[1:3, lead], ref.at[1:3, bottom], UP)
-        send(ref.at[0, 2], ref.at[0, EXT - 2], UP)
+        row_sends.append(send(ref.at[0:2, last], ref.at[0:2, top], DOWN))
+        row_sends.append(send(ref.at[1:3, lead], ref.at[1:3, bottom], UP))
+        row_sends.append(send(ref.at[2, ROWS + 1], ref.at[2, 1], DOWN))
+        row_sends.append(send(ref.at[0, 2], ref.at[0, EXT - 2], UP))
     for ref in (h, m, ga, gb):
-        send(ref.at[last], ref.at[top], DOWN)
-        send(ref.at[lead], ref.at[bottom], UP)
-    send(to_left.at[2], corner_tr, DOWN_LEFT)
-    send(to_right.at[0], corner_bl, UP_RIGHT)
-    send(to_right, from_left, RIGHT)
-    send(to_left, from_right, LEFT)
+        row_sends.append(send(ref.at[last], ref.at[top], DOWN))
+        row_sends.append(send(ref.at[lead], ref.at[bottom], UP))
+    rim_sends.append(send(to_right.at[0], corner_bl, UP_RIGHT))
+    rim_sends.append(send(to_right, from_left, RIGHT))
 
     def invert(row):
         return [1.0 / ga[row, :, tile(t)] for t in range(2)]
@@ -343,9 +354,11 @@
 
     staged(range(2, ROWS + 2), invert, keep, 8)
     turned_rows(range(2, ROWS + 2), v, h, w, m, ga, turned)
-    pl.semaphore_wait(corner_sem, 1)
-    send(to_left.at[0], corner_br, UP_LEFT)
     energy_rows(range(3, ROWS + 1), v, w, ga, gb, inverse, kin)
+    pl.semaphore_wait(left_sem, 1)
+    rim_sends.append(send(to_left.at[2], corner_tr, DOWN_LEFT))
+    rim_sends.append(send(to_left, from_right, LEFT))
+    rim_sends.append(send(to_left.at[0], corner_br, UP_LEFT))
 
     def group(index, _):
         base = 3 + index * GROUP
@@ -355,7 +368,24 @@
     lax.fori_loop(0, (ROWS - 2) // GROUP, group, 0)
     cell_rows(range(4, ROWS), sums, cell)
 
-    for copy in sends:
+    for copy in row_sends:
+        copy.wait_recv()
+    turned_rows((0, 1, EXT - 2, EXT - 1), v, h, w, m, ga, turned)
+    vertex_rows([(e, e) for e in (0, 1, 2, ROWS + 1, ROWS + 2, ROWS + 3)], v, h, w, m, ga, gb, turned, sums, 2, EXT - 1, 0)
+    energy_rows((2, ROWS + 1), v, w, ga, gb, inverse, kin)
+    cell_rows((1, 2, 3, ROWS, ROWS + 1, ROWS + 2), sums, cell)
+    merged = {}
+    for b in range(3):
+        for f in range(FIELDS):
+            x = own[f, b]
+            for r in ((-2, -1) if b == 0 else ((32, 33) if b == 2 else ())):
+                q = (r - FIRST[b]) * 8
+                x = jnp.where((lane >= q) & (lane < q + 4), turn(strip(f, r + 2), q - 126), x)
+            merged[f, b] = jnp.where(slot < 2, x, turn(x, 3))
+    for (f, b), x in merged.items():
+        own[f, b] = x
+
+    for copy in rim_sends:
         copy.wait_recv()
 
     top_rows, bottom_rows = lane < 16, (lane >= 48) & (lane < 64)
@@ -369,14 +399,9 @@
             right = [jnp.where(bottom_rows, turn(corner_br[s], 32), right[s]) for s in range(3)]
             left = [jnp.where(bottom_rows, turn(corner_bl[s], 32), left[s]) for s in range(2)]
         for f in range(FIELDS):
-            x = own[f, b]
-            for r in ((-2, -1) if b == 0 else ((32, 33) if b == 2 else ())):
-                q = (r - FIRST[b]) * 8
-                x = jnp.where((lane >= q) & (lane < q + 4), turn(strip(f, r + 2), q - 126), x)
             y = turn(right[f // 4], 2 - 2 * (f % 4))
             z = turn(left[f // 8], 4 - f % 8)
-            strips[f, b] = jnp.where(slot < 2, x, jnp.where(slot < 4, y, jnp.where(slot == 4, z, turn(x, 3))))
-    turned_rows((0, 1, EXT - 2, EXT - 1), v, h, w, m, ga, turned)
+            strips[f, b] = jnp.where((slot >> 1) == 1, y, jnp.where(slot == 4, z, own[f, b]))
     for (f, b), x in strips.items():
         rim[f, b] = x
 
@@ -417,9 +442,6 @@
     for (which, n, b), x in results.items():
         (rim_patch, rim_c, rim_right)[which][n, b] = x
 
-    vertex_rows([(e, e) for e in (0, 1, 2, ROWS + 1, ROWS + 2, ROWS + 3)], v, h, w, m, ga, gb, turned, sums, 2, EXT - 1, 0)
-    energy_rows((2, ROWS + 1), v, w, ga, gb, inverse, kin)
-    cell_rows((1, 2, 3, ROWS, ROWS + 1, ROWS + 2), sums, cell)
     for copy in sends:
         copy.wait_send()
 
@@ -442,44 +464,58 @@
         copies.append(pltpu.make_async_copy(src, dst, sem.at[len(copies)]))
         copies[-1].start()
 
-    def begin(r):
+    def begin_patch(r):
+        values = [row_pair(sums, 0, r + 2), pick(rim_patch, 0, r, 0, LANES - 1)]
+        if r >= 0:
+            values += [row_pair(sums, 2, r + 2), row_pair(kin, r), pick(rim_patch, 1, r, 0, LANES - 1)]
+        return values
+
+    def finish_patch(r, values):
+        v0, patch = values[0:2]
+        vertex_buf[0, r + 1, :, tile(0)] = v0[0]
+        vertex_buf[0, r + 1, :, tile(1)] = jnp.where(is_last, patch, v0[1])
+        if r >= 0:
+            v1, energy, other = values[2:5]
+            kinetic_buf[r, :, tile(0)] = jnp.where(is_first, patch, energy[0])
+            kinetic_buf[r, :, tile(1)] = energy[1]
+            vertex_buf[1, r + 1, :, tile(0)] = v1[0]
+            vertex_buf[1, r + 1, :, tile(1)] = jnp.where(is_last, other, v1[1])
+            corner_buf[r, :, tile(0)] = other
+
+    staged(range(-1, ROWS), begin_patch, finish_patch, 8)
+    for k in range(LEVELS):
+        put(vertex_buf.at[:, 1 : ROWS + 1, k], vertex_out.at[:, k])
+        put(kinetic_buf.at[:, k], kinetic_out.at[k])
+
+    def begin_cell(r):
         values = []
         for n in range(2):
             pair = row_pair(cell, n, r + 2)
             values += [pair, turn(pair[0], -1), turn(pair[1], -1), pick(rim_c, n, r, 0, LANES - 1), pick(rim_right, n, r, 1, LANES - 2)]
-        if r < ROWS:
-            values += [row_pair(sums, 0, r + 2), pick(rim_patch, 0, r, 0, LANES - 1)]
-            if r >= 0:
-                values += [row_pair(sums, 2, r + 2), row_pair(kin, r), pick(rim_patch, 1, r, 0, LANES - 1)]
-                below = row_pair(sums, 2, r + 3)
-                values += [turn(below[0], 1), turn(below[1], 1)]
         return values
 
-    def finish(r, values):
+    def finish_cell(r, values):
         for n, buf in ((0, cell_buf), (1, other_buf)):
             pair, first, second, patch, patch_right = values[5 * n : 5 * n + 5]
             buf[r + 1, :, tile(0)] = jnp.where(is_first, patch, pair[0])
             buf[r + 1, :, tile(1)] = jnp.where(is_last, patch, pair[1])
             right_buf[n, r + 1, :, tile(0)] = jnp.where(is_last, second, first)
             right_buf[n, r + 1, :, tile(1)] = jnp.where(tail, patch_right, second)
-        if r < ROWS:
-            v0, patch = values[10:12]
-            vertex_buf[0, r + 1, :, tile(0)] = v0[0]
-            vertex_buf[0, r + 1, :, tile(1)] = jnp.where(is_last, patch, v0[1])
-            if r >= 0:
-                v1, energy, other, first, second = values[12:17]
-                kinetic_buf[r, :, tile(0)] = jnp.where(is_first, patch, energy[0])
-                kinetic_buf[r, :, tile(1)] = energy[1]
-                vertex_buf[1, r + 1, :, tile(0)] = v1[0]
-                vertex_buf[1, r + 1, :, tile(1)] = jnp.where(is_last, other, v1[1])
-                corner_buf[r, :, tile(0)] = jnp.where(is_first, other, first)
-                corner_buf[r, :, tile(1)] = jnp.where(is_first, first, second)
-
-    staged(range(-1, ROWS + 1), begin, finish, 8)
+
+    staged(range(-1, ROWS + 1), begin_cell, finish_cell, 8)
     for k in range(LEVELS):
-        put(vertex_buf.at[:, 1 : ROWS + 1, k], vertex_out.at[:, k])
-        put(kinetic_buf.at[:, k], kinetic_out.at[k])
         put(cell_buf.at[1 : ROWS + 1, k], cell_out.at[k])
+
+    def begin_corner(r):
+        below = row_pair(sums, 2, r + 3)
+        return turn(below[0], 1), turn(below[1], 1), corner_buf[r, :, tile(0)]
+
+    def finish_corner(r, values):
+        first, second, other = values
+        corner_buf[r, :, tile(0)] = jnp.where(is_first, other, first)
+        corner_buf[r, :, tile(1)] = jnp.where(is_first, first, second)
+
+    staged(range(ROWS), begin_corner, finish_corner, 8)
 
     def slopes(r):
         v0, v1 = row_pair(vertex_buf, 0, r + 1), row_pair(vertex_buf, 1, r + 1)
@@ -506,10 +542,11 @@
             for t in range(2):
                 edge_buf[k, r, :, tile(t)] = values[2 * k + t]
 
-    half = ROWS // 2
-    for part in range(2):
-        rows = pl.ds(part * half, half)
-        staged(range(part * half, (part + 1) * half), slopes, keep, 3)
+    parts = 2
+    size = ROWS // parts
+    for part in range(parts):
+        rows = pl.ds(part * size, size)
+        staged(range(part * size, (part + 1) * size), slopes, keep, 3)
         for k in range(LEVELS):
             put(edge_buf.at[:, rows, k], edge_out.at[:, k, rows])
     for copy in copies:
@@ -556,7 +593,7 @@
                 pltpu.VMEM((2, ROWS + 1, *wide), F32), pltpu.VMEM((ROWS, *wide), F32),
                 pltpu.VMEM((ROWS + 2, *wide), F32), pltpu.VMEM((3, ROWS, *wide), F32),
                 pltpu.VMEM((ROWS + 2, *wide), F32), pltpu.VMEM((2, ROWS + 2, *wide), F32), pltpu.VMEM((ROWS, *wide), F32),
-                pltpu.SemaphoreType.DMA((64,)),
+                pltpu.SemaphoreType.DMA((40,)),
             ],
             compiler_params=pltpu.CompilerParams(vmem_limit_bytes=grant),
         )(*between)

time: 17.1 us -> 16.3 us (0.953)
  Pallas kernels: 16.3 us -> 15.4 us
    pallas_call x1, Pallas kernels: 14.1 us -> 13.4 us  [local(): pl.pallas_call(exchange_kernel, out_shape=[pltpu.VMEM(s, F32) for s in pa...]
    pallas_call x1, Pallas kernels: 2.2 us -> 2.01 us  [local(): pl.pallas_call(output_kernel, out_shape=[jax.ShapeDtypeStruct(s, F32) for...]
where the time goes in v4:
time: 16.3 us; the launch traced here: 16.1 us
  Pallas kernels  15.4 us (94%)
  between operations  0.64 us (4%)
    pallas_call x1, Pallas kernels, local(): pl.pallas_call(exchange_kernel, out_shape=[pltpu.VMEM(s, F32) for s in pa...  13.4 us
    pallas_call x1, Pallas kernels, local(): pl.pallas_call(output_kernel, out_shape=[jax.ShapeDtypeStruct(s, F32) for...  2.01 us

profile of v4, /device:TPU:0, one launch (start us, length us, event | category | flops | bytes accessed | tf_op | source)
XLA Modules:
  0.0 16.1 jit_solution(12508199464508021396)
XLA Ops:
  0.6 13.4 %shard_map.120 = (f32[3,36,8,256]{3,2,1,0:T(8,128)S(1)}, f32[3,36,8,256]{3,2,1,0:T(8,128)S(1)}, f32[4,36,8,256]{3,2,1,0:T(8,128)S(1)}, f32[2,36,8,256]{3,2,1,0:T...) custom-call(f32[3,8,32,256]{3,2,1,0:T(8,128)} %v_in.1, ...), custom_call_target="tpu_custom_call" | custom-call | tf_op jit(solution)/shard_map/pallas_call | solution.py:567
  14.1 2.0 %shard_map.121 = (f32[2,8,32,256]{3,2,1,0:T(8,128)}, f32[8,32,256]{2,1,0:T(8,128)}, f32[8,32,256]{2,1,0:T(8,128)}, f32[3,8,32,256]{3,2,1,0:T(8,128)}) custom-call(f32[3,36,8,256]{3,2,1,0:T(8,128)S(1)} %get-tuple-element.13.v, f32[3,36,8,256]{3,2,1,0:T(8,128)S(1)} %get-tuple-element.14.w, f32[4,36,8,256]{3,2,1,0:T(8,128)S(1)} %get-tuple-element.15.sums, ...), custom_call_target="tpu_custom_call" | custom-call | tf_op jit(solution)/shard_map/pallas_call | solution.py:587

commit v5 on v4

--- a/solution.py
+++ b/solution.py
@@ -193,6 +193,28 @@
     staged(rows, begin, finish, 5)
 
 
+def side_rows(cell_at, vertex_at, cell, sums, right, corner):
+    def begin(item):
+        ref, row, back = item
+        pair = row_pair(*ref, row)
+        amount = 1 if back else -1
+        return turn(pair[0], amount), turn(pair[1], amount)
+
+    def finish(item, values):
+        (_, n), row, back = item
+        lane = lane_id()
+        if back:
+            corner[row - 3, :, tile(0)] = values[0]
+            corner[row - 3, :, tile(1)] = jnp.where(lane == 0, values[0], values[1])
+        else:
+            right[n, row - 1, :, tile(0)] = jnp.where(lane == LANES - 1, values[1], values[0])
+            right[n, row - 1, :, tile(1)] = values[1]
+
+    items = [((sums, 2), row, True) for row in vertex_at]
+    items += [((cell, n), row, False) for row in cell_at for n in range(2)]
+    staged(items, begin, finish, 12)
+
+
 def energy_rows(rows, v, w, ga, gb, inverse, out):
     spots = ((ga, 6), (ga, 7), (gb, 6))
     known = {}
@@ -223,7 +245,7 @@
 
 def exchange_kernel(
     v_in, h_in, w_in, m_in, cd_in, el_in, ca_in, ka_in, co_in,
-    v, w, sums, cell, kin, inverse, rim_patch, rim_c, rim_right,
+    v, w, sums, cell, kin, inverse, side, corner, rim_patch, rim_c, rim_right,
     h, m, ga, gb, turned, own, to_right, to_left, from_left, from_right, corner_tr, corner_br, corner_bl, rim,
     load_sem, send_sem, recv_sem, left_sem,
 ):
@@ -287,8 +309,8 @@
         return jnp.where(lane >= 64, field(f, e, 1), field(f, e, 0))
 
     total = {}
-    for step, fields in enumerate(((8, 9), (6, 7), (0, 1, 2), (3, 4, 5))):
-        arrived(step)
+
+    def gather(fields):
         for b in (2, 0, 1):
             rows = [r for r in range(FIRST[b], FIRST[b] + 16) if 0 <= r < ROWS]
             masks = [(lane >= (r - FIRST[b]) * 8) & (lane < (r - FIRST[b]) * 8 + 4) for r in rows]
@@ -297,6 +319,43 @@
                 for r, mask in zip(rows, masks):
                     x = jnp.where(mask, turn(strip(f, r + 2), (r - FIRST[b]) * 8 - 126), x)
                 total[f, b] = x
+
+    arrived(0)
+    gather((8, 9))
+    arrived(1)
+    gather((6, 7))
+    arrived(2)
+    arrived(3)
+
+    pl.semaphore_wait(barrier, 4)
+    tell(left_sem, RIGHT)
+
+    sends = []
+
+    def send(src, dst, target):
+        n = len(sends)
+        sends.append(
+            pltpu.make_async_remote_copy(
+                src_ref=src, dst_ref=dst, send_sem=send_sem.at[n], recv_sem=recv_sem.at[n],
+                device_id=device(*target), device_id_type=MESH,
+            )
+        )
+        sends[-1].start()
+        return sends[-1]
+
+    top, bottom = pl.ds(0, 2), pl.ds(EXT - 2, 2)
+    last, lead = pl.ds(ROWS, 2), pl.ds(2, 2)
+    row_sends, rim_sends = [], []
+    for ref in (v, w):
+        row_sends.append(send(ref.at[0:2, last], ref.at[0:2, top], DOWN))
+        row_sends.append(send(ref.at[1:3, lead], ref.at[1:3, bottom], UP))
+        row_sends.append(send(ref.at[2, ROWS + 1], ref.at[2, 1], DOWN))
+        row_sends.append(send(ref.at[0, 2], ref.at[0, EXT - 2], UP))
+    for ref in (h, m, ga, gb):
+        row_sends.append(send(ref.at[last], ref.at[top], DOWN))
+        row_sends.append(send(ref.at[lead], ref.at[bottom], UP))
+    gather((0, 1, 2))
+    gather((3, 4, 5))
     packs = {}
     for b in (2, 0, 1):
         for s in range(3):
@@ -315,36 +374,6 @@
     for (f, b), x in total.items():
         own[f, b] = x
 
-    pl.semaphore_wait(barrier, 4)
-    tell(left_sem, RIGHT)
-
-    sends = []
-
-    def send(src, dst, target):
-        n = len(sends)
-        sends.append(
-            pltpu.make_async_remote_copy(
-                src_ref=src, dst_ref=dst, send_sem=send_sem.at[n], recv_sem=recv_sem.at[n],
-                device_id=device(*target), device_id_type=MESH,
-            )
-        )
-        sends[-1].start()
-        return sends[-1]
-
-    top, bottom = pl.ds(0, 2), pl.ds(EXT - 2, 2)
-    last, lead = pl.ds(ROWS, 2), pl.ds(2, 2)
-    row_sends, rim_sends = [], []
-    for ref in (v, w):
-        row_sends.append(send(ref.at[0:2, last], ref.at[0:2, top], DOWN))
-        row_sends.append(send(ref.at[1:3, lead], ref.at[1:3, bottom], UP))
-        row_sends.append(send(ref.at[2, ROWS + 1], ref.at[2, 1], DOWN))
-        row_sends.append(send(ref.at[0, 2], ref.at[0, EXT - 2], UP))
-    for ref in (h, m, ga, gb):
-        row_sends.append(send(ref.at[last], ref.at[top], DOWN))
-        row_sends.append(send(ref.at[lead], ref.at[bottom], UP))
-    rim_sends.append(send(to_right.at[0], corner_bl, UP_RIGHT))
-    rim_sends.append(send(to_right, from_left, RIGHT))
-
     def invert(row):
         return [1.0 / ga[row, :, tile(t)] for t in range(2)]
 
@@ -353,6 +382,9 @@
             inverse[row, :, tile(t)] = values[t]
 
     staged(range(2, ROWS + 2), invert, keep, 8)
+    rim_sends.append(send(to_right.at[0], corner_bl, UP_RIGHT))
+    rim_sends.append(send(to_right, from_left, RIGHT))
+
     turned_rows(range(2, ROWS + 2), v, h, w, m, ga, turned)
     energy_rows(range(3, ROWS + 1), v, w, ga, gb, inverse, kin)
     pl.semaphore_wait(left_sem, 1)
@@ -367,6 +399,7 @@
 
     lax.fori_loop(0, (ROWS - 2) // GROUP, group, 0)
     cell_rows(range(4, ROWS), sums, cell)
+    side_rows(range(4, ROWS), range(3, ROWS + 1), cell, sums, side, corner)
 
     for copy in row_sends:
         copy.wait_recv()
@@ -374,6 +407,7 @@
     vertex_rows([(e, e) for e in (0, 1, 2, ROWS + 1, ROWS + 2, ROWS + 3)], v, h, w, m, ga, gb, turned, sums, 2, EXT - 1, 0)
     energy_rows((2, ROWS + 1), v, w, ga, gb, inverse, kin)
     cell_rows((1, 2, 3, ROWS, ROWS + 1, ROWS + 2), sums, cell)
+    side_rows((1, 2, 3, ROWS, ROWS + 1), (ROWS + 1, ROWS + 2), cell, sums, side, corner)
     merged = {}
     for b in range(3):
         for f in range(FIELDS):
@@ -447,9 +481,9 @@
 
 
 def output_kernel(
-    v, w, sums, cell, kin, inverse, rim_patch, rim_c, rim_right,
+    v, w, sums, cell, kin, inverse, side, corner, rim_patch, rim_c, rim_right,
     vertex_out, kinetic_out, cell_out, edge_out,
-    vertex_buf, kinetic_buf, cell_buf, edge_buf, other_buf, right_buf, corner_buf, sem,
+    vertex_buf, kinetic_buf, cell_buf, edge_buf, corner_buf, sem,
 ):
     lane = lane_id()
     is_last, is_first, tail = lane == LANES - 1, lane == 0, lane >= LANES - 2
@@ -480,75 +514,67 @@
             kinetic_buf[r, :, tile(1)] = energy[1]
             vertex_buf[1, r + 1, :, tile(0)] = v1[0]
             vertex_buf[1, r + 1, :, tile(1)] = jnp.where(is_last, other, v1[1])
-            corner_buf[r, :, tile(0)] = other
+            corner_buf[r] = other
 
     staged(range(-1, ROWS), begin_patch, finish_patch, 8)
     for k in range(LEVELS):
         put(vertex_buf.at[:, 1 : ROWS + 1, k], vertex_out.at[:, k])
         put(kinetic_buf.at[:, k], kinetic_out.at[k])
 
-    def begin_cell(r):
-        values = []
-        for n in range(2):
+    def begin(r):
+        picks = [(pick(rim_c, n, r, 0, LANES - 1), pick(rim_right, n, r, 1, LANES - 2)) for n in range(2)]
+        return picks
+
+    cells, sides = {}, {}
+
+    def work(r, picks):
+        stores = []
+        cells[r] = []
+        sides[r] = []
+        for n, (patch, patch_side) in enumerate(picks):
             pair = row_pair(cell, n, r + 2)
-            values += [pair, turn(pair[0], -1), turn(pair[1], -1), pick(rim_c, n, r, 0, LANES - 1), pick(rim_right, n, r, 1, LANES - 2)]
-        return values
-
-    def finish_cell(r, values):
-        for n, buf in ((0, cell_buf), (1, other_buf)):
-            pair, first, second, patch, patch_right = values[5 * n : 5 * n + 5]
-            buf[r + 1, :, tile(0)] = jnp.where(is_first, patch, pair[0])
-            buf[r + 1, :, tile(1)] = jnp.where(is_last, patch, pair[1])
-            right_buf[n, r + 1, :, tile(0)] = jnp.where(is_last, second, first)
-            right_buf[n, r + 1, :, tile(1)] = jnp.where(tail, patch_right, second)
-
-    staged(range(-1, ROWS + 1), begin_cell, finish_cell, 8)
-    for k in range(LEVELS):
-        put(cell_buf.at[1 : ROWS + 1, k], cell_out.at[k])
-
-    def begin_corner(r):
-        below = row_pair(sums, 2, r + 3)
-        return turn(below[0], 1), turn(below[1], 1), corner_buf[r, :, tile(0)]
-
-    def finish_corner(r, values):
-        first, second, other = values
-        corner_buf[r, :, tile(0)] = jnp.where(is_first, other, first)
-        corner_buf[r, :, tile(1)] = jnp.where(is_first, first, second)
-
-    staged(range(ROWS), begin_corner, finish_corner, 8)
-
-    def slopes(r):
-        v0, v1 = row_pair(vertex_buf, 0, r + 1), row_pair(vertex_buf, 1, r + 1)
-        means = (
-            both(add, v0, row_pair(corner_buf, r)),
-            both(add, v0, v1),
-            both(add, v1, row_pair(vertex_buf, 0, r)),
-        )
-        here = (row_pair(cell_buf, r + 1), row_pair(other_buf, r + 1))
-        lower = (row_pair(cell_buf, r + 2), row_pair(other_buf, r + 2))
-        right = (row_pair(right_buf, 0, r + 1), row_pair(right_buf, 1, r + 1))
-        upper = (row_pair(right_buf, 0, r), row_pair(right_buf, 1, r))
-        values = []
-        for k, side in enumerate((lower, right, upper)):
-            velocity, tendency = row_pair(v, k, r + 2), row_pair(w, k, r + 2)
-            factor = spread_pair(inverse, r + 2, k)
-            for t in range(2):
-                slope = velocity[t] * (side[0][t] - here[0][t]) + tendency[t] * (side[1][t] - here[1][t])
-                values.append(0.5 * (means[k][t] - slope * factor[t]))
-        return values
-
-    def keep(r, values):
-        for k in range(3):
-            for t in range(2):
-                edge_buf[k, r, :, tile(t)] = values[2 * k + t]
-
-    parts = 2
-    size = ROWS // parts
-    for part in range(parts):
-        rows = pl.ds(part * size, size)
-        staged(range(part * size, (part + 1) * size), slopes, keep, 3)
-        for k in range(LEVELS):
-            put(edge_buf.at[:, rows, k], edge_out.at[:, k, rows])
+            cells[r].append((jnp.where(is_first, patch, pair[0]), jnp.where(is_last, patch, pair[1])))
+            if r < ROWS:
+                pair = row_pair(side, n, r + 1)
+                sides[r].append((pair[0], jnp.where(tail, patch_side, pair[1])))
+        if 0 <= r < ROWS:
+            stores += [(cell_buf, (r,), t, cells[r][0][t]) for t in range(2)]
+        q = r - 1
+        if q >= 0:
+            v0, v1, above = row_pair(vertex_buf, 0, q + 1), row_pair(vertex_buf, 1, q + 1), row_pair(vertex_buf, 0, q)
+            back = row_pair(corner, q)
+            means = (both(add, v0, (jnp.where(is_first, corner_buf[q], back[0]), back[1])), both(add, v0, v1), both(add, v1, above))
+            here = cells[q]
+            for k, other in enumerate((cells[r], sides[q], sides[q - 1])):
+                velocity, tendency = row_pair(v, k, q + 2), row_pair(w, k, q + 2)
+                factor = spread_pair(inverse, q + 2, k)
+                for t in range(2):
+                    slope = velocity[t] * (other[0][t] - here[0][t]) + tendency[t] * (other[1][t] - here[1][t])
+                    stores.append((edge_buf, (k, q), t, 0.5 * (means[k][t] - slope * factor[t])))
+        return stores
+
+    def keep(stores):
+        for ref, index, t, value in stores:
+            ref[(*index, slice(None), tile(t))] = value
+
+    half = ROWS // 2
+    rows = list(range(-1, ROWS + 1))
+    ahead = {r: begin(r) for r in rows[:8]}
+    behind = []
+    for r in rows:
+        if r + 8 <= ROWS:
+            ahead[r + 8] = begin(r + 8)
+        behind.append(work(r, ahead.pop(r)))
+        if len(behind) > 2:
+            keep(behind.pop(0))
+        if r in (half, ROWS):
+            while behind:
+                keep(behind.pop(0))
+            part = pl.ds(r - half, half)
+            for k in range(LEVELS):
+                put(edge_buf.at[:, part, k], edge_out.at[:, k, part])
+            for k in range(LEVELS):
+                put(cell_buf.at[part, k], cell_out.at[k, part])
     for copy in copies:
         copy.wait()
 
@@ -561,6 +587,7 @@
     thin = (LEVELS, LANES)
     passed = [
         (3, EXT, *wide), (3, EXT, *wide), (4, EXT, *wide), (2, EXT, *wide), (ROWS, *wide), (EXT, *wide),
+        (2, ROWS + 1, *wide), (ROWS, *wide),
         (2, 3, *thin), (2, 3, *thin), (2, 3, *thin),
     ]
     grant = 24 << 20
@@ -591,9 +618,8 @@
             out_specs=[anywhere] * 4,
             scratch_shapes=[
                 pltpu.VMEM((2, ROWS + 1, *wide), F32), pltpu.VMEM((ROWS, *wide), F32),
-                pltpu.VMEM((ROWS + 2, *wide), F32), pltpu.VMEM((3, ROWS, *wide), F32),
-                pltpu.VMEM((ROWS + 2, *wide), F32), pltpu.VMEM((2, ROWS + 2, *wide), F32), pltpu.VMEM((ROWS, *wide), F32),
-                pltpu.SemaphoreType.DMA((40,)),
+                pltpu.VMEM((ROWS, *wide), F32), pltpu.VMEM((3, ROWS, *wide), F32), pltpu.VMEM((ROWS, *thin), F32),
+                pltpu.SemaphoreType.DMA((48,)),
             ],
             compiler_params=pltpu.CompilerParams(vmem_limit_bytes=grant),
         )(*between)

time: 16.3 us -> 15.7 us (0.963)
  Pallas kernels: 15.4 us -> 14.8 us
    pallas_call x1, Pallas kernels: 13.4 us -> 12.9 us  [local(): pl.pallas_call(exchange_kernel, out_shape=[pltpu.VMEM(s, F32) for s in pa...]
where the time goes in v5:
time: 15.7 us; the launch traced here: 15.5 us
  Pallas kernels  14.8 us (94%)
  between operations  0.64 us (4%)
    pallas_call x1, Pallas kernels, local(): pl.pallas_call(exchange_kernel, out_shape=[pltpu.VMEM(s, F32) for s in pa...  12.9 us
    pallas_call x1, Pallas kernels, local(): pl.pallas_call(output_kernel, out_shape=[jax.ShapeDtypeStruct(s, F32) for...  1.89 us

profile of v5, /device:TPU:0, one launch (start us, length us, event | category | flops | bytes accessed | tf_op | source)
XLA Modules:
  0.0 15.5 jit_solution(10243149935730987655)
XLA Ops:
  0.6 12.9 %shard_map.120 = (f32[3,36,8,256]{3,2,1,0:T(8,128)S(1)}, f32[3,36,8,256]{3,2,1,0:T(8,128)S(1)}, f32[4,36,8,256]{3,2,1,0:T(8,128)S(1)}, f32[2,36,8,256]{3,2,1,0:T...) custom-call(f32[3,8,32,256]{3,2,1,0:T(8,128)} %v_in.1, ...), custom_call_target="tpu_custom_call" | custom-call | tf_op jit(solution)/shard_map/pallas_call | solution.py:594
  13.6 1.9 %shard_map.121 = (f32[2,8,32,256]{3,2,1,0:T(8,128)}, f32[8,32,256]{2,1,0:T(8,128)}, f32[8,32,256]{2,1,0:T(8,128)}, f32[3,8,32,256]{3,2,1,0:T(8,128)}) custom-call(f32[3,36,8,256]{3,2,1,0:T(8,128)S(1)} %get-tuple-element.15.v, f32[3,36,8,256]{3,2,1,0:T(8,128)S(1)} %get-tuple-element.16.w, f32[4,36,8,256]{3,2,1,0:T(8,128)S(1)} %get-tuple-element.17.sums, ...), custom_call_target="tpu_custom_call" | custom-call | tf_op jit(solution)/shard_map/pallas_call | solution.py:614

commit v6 on v5

--- a/solution.py
+++ b/solution.py
@@ -325,6 +325,7 @@
     arrived(1)
     gather((6, 7))
     arrived(2)
+    gather((0, 1, 2))
     arrived(3)
 
     pl.semaphore_wait(barrier, 4)
@@ -354,7 +355,6 @@
     for ref in (h, m, ga, gb):
         row_sends.append(send(ref.at[last], ref.at[top], DOWN))
         row_sends.append(send(ref.at[lead], ref.at[bottom], UP))
-    gather((0, 1, 2))
     gather((3, 4, 5))
     packs = {}
     for b in (2, 0, 1):

time: 15.7 us -> 15.7 us (level)
  no operation moved by 1% of the time
where the time goes in v6:
time: 15.7 us; the launch traced here: 15.5 us
  Pallas kernels  14.8 us (94%)
  between operations  0.64 us (4%)
    pallas_call x1, Pallas kernels, local(): pl.pallas_call(exchange_kernel, out_shape=[pltpu.VMEM(s, F32) for s in pa...  13 us
    pallas_call x1, Pallas kernels, local(): pl.pallas_call(output_kernel, out_shape=[jax.ShapeDtypeStruct(s, F32) for...  1.89 us

profile of v6, /device:TPU:0, one launch (start us, length us, event | category | flops | bytes accessed | tf_op | source)
XLA Modules:
  0.0 15.5 jit_solution(3401596160970822672)
XLA Ops:
  0.6 13.0 %shard_map.120 = (f32[3,36,8,256]{3,2,1,0:T(8,128)S(1)}, f32[3,36,8,256]{3,2,1,0:T(8,128)S(1)}, f32[4,36,8,256]{3,2,1,0:T(8,128)S(1)}, f32[2,36,8,256]{3,2,1,0:T...) custom-call(f32[3,8,32,256]{3,2,1,0:T(8,128)} %v_in.1, ...), custom_call_target="tpu_custom_call" | custom-call | tf_op jit(solution)/shard_map/pallas_call | solution.py:594
  13.6 1.9 %shard_map.121 = (f32[2,8,32,256]{3,2,1,0:T(8,128)}, f32[8,32,256]{2,1,0:T(8,128)}, f32[8,32,256]{2,1,0:T(8,128)}, f32[3,8,32,256]{3,2,1,0:T(8,128)}) custom-call(f32[3,36,8,256]{3,2,1,0:T(8,128)S(1)} %get-tuple-element.15.v, f32[3,36,8,256]{3,2,1,0:T(8,128)S(1)} %get-tuple-element.16.w, f32[4,36,8,256]{3,2,1,0:T(8,128)S(1)} %get-tuple-element.17.sums, ...), custom_call_target="tpu_custom_call" | custom-call | tf_op jit(solution)/shard_map/pallas_call | solution.py:614
